TPU v7x, 256 devices: a whole 4x4x8 slice. The times are simulated.
256 devices in a mesh: expert: 8 (over x, y_lo), tensor: 16 (over y_hi, z), dp: 2 (over core).
Axes of the slice: x: 4, y: 4 (y_hi: 2, y_lo: 2; y = y_hi * 2 + y_lo), z: 8, core: 2. Of those that a mesh axis runs over, the one named last changes fastest.
Arguments:
- x_real: bfloat16 [4096, 2048], P(('expert', 'dp'), 'tensor'), may hold values from -6 to 6
- routes_real: int32 [4096, 2], P(('expert', 'dp')), may hold values from 0 to 7, all different within a row; in each aligned block of 256 rows (0 to 255, 256 to 511, ...) at most 128 rows name the same one
- gates_real: float32 [4096, 2], P(('expert', 'dp')), may hold values from 0.2 to 1
- up_real: bfloat16 [8, 2048, 8192], P('expert', None, 'tensor'), may hold values from -0.125 to 0.125
- down_real: bfloat16 [8, 8192, 2048], P('expert', 'tensor'), may hold values from -0.0625 to 0.0625
- x_fake: bfloat16 [4096, 2048], P(('expert', 'dp'), 'tensor'), may hold values from -6 to 6
- routes_fake: int32 [4096, 2], P(('expert', 'dp')), may hold values from 0 to 7, all different within a row; in each aligned block of 256 rows (0 to 255, 256 to 511, ...) at most 128 rows name the same one
- gates_fake: float32 [4096, 2], P(('expert', 'dp')), may hold values from 0.2 to 1
- cotangent: bfloat16 [4096, 2048], P(('expert', 'dp'), 'tensor'), may hold values from -6 to 6
- up_fake: bfloat16 [8, 2048, 8192], P('expert', None, 'tensor'), may hold values from -0.125 to 0.125
- down_fake: bfloat16 [8, 8192, 2048], P('expert', 'tensor'), may hold values from -0.0625 to 0.0625
Outputs:
- real_out: bfloat16 [4096, 2048], P(('expert', 'dp'), 'tensor')
- grad_up: bfloat16 [8, 2048, 8192], P('expert', 'dp', 'tensor')
- grad_down: bfloat16 [8, 8192, 2048], P('expert', 'tensor', 'dp')
Inputs may be any that keep to these rules, and one draw needn't show every extreme that they name: `routes_real`: each row names 2 different experts. In the 256 rows of one index of expert and dp no expert is named more than 128 times, and that bound is reached. `routes_fake`: each row names 2 different experts. In the 256 rows of one index of expert and dp no expert is named more than 128 times, and that bound is reached.
All inputs are finite; a program needn't handle non-finite values.
Results may differ from a plain program's by a relative error of at most 0.0058.
Values may be sent and summed in bfloat16 or wider, within the bound.
A program may use at most 128 MiB of HBM per device.

v0:
```python
import jax
import jax.numpy as jnp
from jax import lax
from jax.sharding import Mesh
from jax.sharding import PartitionSpec as P

TENSOR = ("tensor_0", "tensor_1")


slope_const = 0.7978845608028654
cubic_coef = 0.044715


def in_order(pieces, dim):
    pieces = jnp.moveaxis(pieces, 0, dim)
    dims = pieces.shape
    return pieces.reshape(*dims[:dim], dims[dim] * dims[dim + 1], *dims[dim + 2 :])


def sent_to_all(x, axis):
    copies = jnp.broadcast_to(x, (lax.axis_size(axis), *x.shape))
    return lax.all_to_all(copies, axis, split_axis=0, concat_axis=0, tiled=True)


def gather_directly(x, axis, dim):
    return in_order(sent_to_all(x, axis), dim)


def reduced_to_own(pieces, axes, turns):
    dims = [lax.axis_size(a) for a in axes]
    pieces = pieces.reshape(*dims, *pieces.shape[1:])
    pieces = pieces.transpose(*turns, *range(len(axes), pieces.ndim))
    pieces = pieces.reshape(-1, *pieces.shape[len(axes) :])
    for k in turns:
        pieces = lax.psum_scatter(pieces, axes[k], scatter_dimension=0, tiled=True)
    return pieces[0]


def in_blocks(x, dim, length):
    dims = x.shape
    pieces = x.reshape(*dims[:dim], length, dims[dim] // length, *dims[dim + 1 :])
    return jnp.moveaxis(pieces, dim, 0)


def sum_by_axis(x, axes, turns, dim):
    length = lax.axis_size(axes)
    return reduced_to_own(in_blocks(x, dim, length), axes, turns)


def sent_together(arrays, axis, dim, along):
    ends, at = ([], 0)
    for a in arrays[:-1]:
        at += a.shape[along]
        ends.append(at)
    both = jnp.concatenate(arrays, axis=along)
    return tuple(jnp.split(lax.all_gather(both, axis, axis=dim, tiled=True), ends, axis=along))


def in_one_piece(arrays, axis, split_dim, concat_dim, along):
    ends, at = ([], 0)
    for a in arrays[:-1]:
        at += a.shape[along]
        ends.append(at)
    both = jnp.concatenate(arrays, axis=along)
    return tuple(
        jnp.split(
            lax.all_to_all(both, axis, split_axis=split_dim, concat_axis=concat_dim, tiled=True),
            ends,
            axis=along,
        )
    )


def partner(value, axis, stride):
    mask = 2**stride
    pairs = [(source, source ^ mask) for source in range(lax.axis_size(axis))]
    return lax.ppermute(value, axis, pairs)


def gelu_tanh(value):
    return (
        0.5 * value * (1.0 + jnp.tanh(slope_const * (value + cubic_coef * value * value * value)))
    )


def gelu_slope(value):
    inner = jnp.tanh(slope_const * (value + cubic_coef * value * value * value))
    return 0.5 * (1.0 + inner) + 0.5 * value * (1.0 - inner * inner) * slope_const * (
        1.0 + 3.0 * cubic_coef * value * value
    )


def slot_index(routes, experts, capacity):
    labels = jnp.arange(experts, dtype=jnp.int32)
    hits = (routes[:, :, None] == labels[None, None, :]).astype(jnp.int32)
    per_token = jnp.sum(hits, axis=1)
    before = jnp.cumsum(per_token, axis=0) - per_token
    slots = jnp.sum(hits * before[:, None, :], axis=2)
    return routes * capacity + slots


def spread_matrix(position, total):
    columns = jnp.arange(total, dtype=jnp.int32)
    match = (position[:, :, None] == columns[None, None, :]).astype(jnp.float32)
    return jnp.sum(match, axis=1).astype(jnp.bfloat16)


def pick_matrix(position, total):
    columns = jnp.arange(total, dtype=jnp.int32)
    flat = position.reshape(-1)
    return (flat[:, None] == columns[None, :]).astype(jnp.bfloat16)


def to_slots(matrix, rows):
    return lax.dot_general(
        matrix, rows, (((0,), (0,)), ((), ())), preferred_element_type=jnp.float32
    )


def over_rows(left, right):
    return lax.dot_general(
        left, right, (((0,), (0,)), ((), ())), preferred_element_type=jnp.float32
    )


def scale_rows(gates, rows):
    scaled = gates[:, :, None] * rows[:, None, :].astype(jnp.float32)
    return scaled.astype(jnp.bfloat16).reshape(-1, rows.shape[1])


def on_device(
    x_real,
    routes_real,
    gates_real,
    up_real,
    down_real,
    x_fake,
    routes_fake,
    gates_fake,
    cotangent,
    up_fake,
    down_fake,
):
    experts = lax.axis_size("expert")
    tokens = x_real.shape[0]
    top = routes_real.shape[1]
    capacity = tokens // 2
    total = experts * capacity
    w_up = up_real[0]
    w_down = down_real[0]
    real_pos = slot_index(routes_real, experts, capacity)
    real_pick = spread_matrix(real_pos, total)
    whole = gather_directly(x_real, TENSOR, 1)
    sent = (
        to_slots(real_pick, whole).astype(jnp.bfloat16).reshape(experts, capacity, whole.shape[1])
    )
    arrived = lax.all_to_all(sent, "expert", split_axis=0, concat_axis=0, tiled=True)
    rows = arrived.reshape(total, arrived.shape[2])
    pre_real = jnp.dot(rows, w_up, preferred_element_type=jnp.float32)
    hidden = gelu_tanh(pre_real).astype(jnp.bfloat16)
    partial_out = jnp.dot(hidden, w_down, preferred_element_type=jnp.float32)
    summed = sum_by_axis(partial_out, TENSOR, (1, 0), 1).astype(jnp.bfloat16)
    returned = lax.all_to_all(
        summed.reshape(experts, capacity, summed.shape[1]),
        "expert",
        split_axis=0,
        concat_axis=0,
        tiled=True,
    )
    returned = returned.reshape(total, returned.shape[2])
    real_flat = pick_matrix(real_pos, total)
    picked = jnp.dot(real_flat, returned, preferred_element_type=jnp.float32).reshape(
        tokens, top, returned.shape[1]
    )
    real_out = jnp.sum(gates_real[:, :, None] * picked, axis=1).astype(jnp.bfloat16)
    fake_pos = slot_index(routes_fake, experts, capacity)
    fake_pick = spread_matrix(fake_pos, total)
    fake_flat = pick_matrix(fake_pos, total)
    whole_x, whole_c = sent_together((x_fake, cotangent), TENSOR, 1, 0)
    width = whole_x.shape[1]
    sent_x = to_slots(fake_pick, whole_x).astype(jnp.bfloat16).reshape(experts, capacity, width)
    sent_d = (
        to_slots(fake_flat, scale_rows(gates_fake, whole_c))
        .astype(jnp.bfloat16)
        .reshape(experts, capacity, width)
    )
    got_x, got_d = in_one_piece((sent_x, sent_d), "expert", 0, 0, 1)
    rows_x = got_x.reshape(total, width)
    rows_d = got_d.reshape(total, width)
    wf_up = up_fake[0]
    wf_down = down_fake[0]
    pre_fake = jnp.dot(rows_x, wf_up, preferred_element_type=jnp.float32)
    act = gelu_tanh(pre_fake).astype(jnp.bfloat16)
    back_act = lax.dot_general(
        rows_d, wf_down, (((1,), (1,)), ((), ())), preferred_element_type=jnp.float32
    )
    dpre = (back_act * gelu_slope(pre_fake)).astype(jnp.bfloat16)
    mine = lax.axis_index("dp")
    half = rows_x.shape[1] // 2
    own_x = lax.dynamic_slice_in_dim(rows_x, mine * half, half, 1)
    other_x = lax.dynamic_slice_in_dim(rows_x, (1 - mine) * half, half, 1)
    own_d = lax.dynamic_slice_in_dim(rows_d, mine * half, half, 1)
    other_d = lax.dynamic_slice_in_dim(rows_d, (1 - mine) * half, half, 1)
    peer_x, peer_d, peer_act, peer_dpre = partner((other_x, other_d, act, dpre), "dp", 0)
    grad_in = over_rows(own_x, dpre) + over_rows(peer_x, peer_dpre)
    grad_out = over_rows(act, own_d) + over_rows(peer_act, peer_d)
    return (real_out, grad_in.astype(jnp.bfloat16)[None], grad_out.astype(jnp.bfloat16)[None])


def solution(mesh):
    split = Mesh(
        mesh.devices.reshape(mesh.shape["expert"], 2, 8, mesh.shape["dp"]),
        ("expert", "tensor_0", "tensor_1", "dp"),
    )
    placed = (
        P(("expert", "dp"), TENSOR),
        P(("expert", "dp"), None),
        P(("expert", "dp"), None),
        P("expert", None, TENSOR),
        P("expert", TENSOR, None),
        P(("expert", "dp"), TENSOR),
        P(("expert", "dp"), None),
        P(("expert", "dp"), None),
        P(("expert", "dp"), TENSOR),
        P("expert", None, TENSOR),
        P("expert", TENSOR, None),
    )
    return jax.shard_map(
        on_device,
        mesh=split,
        in_specs=placed,
        out_specs=(
            P(("expert", "dp"), TENSOR),
            P("expert", "dp", TENSOR),
            P("expert", TENSOR, "dp"),
        ),
        check_vma=False,
    )
```

profile of v0, /device:TPU:6, one launch (start us, length us, event | category | flops | bytes accessed | tf_op | source)
XLA Modules:
  0.0 412.9 jit_solution(13704326496032141894)
XLA Ops:
  8.0 1.1 copy.30
  9.1 1.1 broadcast_in_dim.6
  10.2 11.2 %all-to-all-start = ((bf16[16,256,128]{1,2,0:T(8,128)(2,1)}), bf16[16,256,128]{1,2,0:T(8,128)(2,1)S(1)}, u32[]{:S(2)}, u32[]{:S(2)}) async-start(bf16[16,256,128]{1,2,0:T(8,128)(2,1)} %broadcast_in_dim.6), calls=%async_computation | async-start | bytes 2097152 | tf_op jit(solution)/shard_map/all_to_all | solution.py:22
  21.4 0.6 reduce-window.14
  22.0 0.2 slice_reduce_fusion.1
  22.4 1.1 convert_reduce_fusion.1
  23.4 26.6 %all-to-all-done = bf16[16,256,128]{1,2,0:T(8,128)(2,1)S(1)} async-done(((bf16[16,256,128]{1,2,0:T(8,128)(2,1)}), bf16[16,256,128]{1,2,0:T(8,128)(2,1)S(1)}, u32[]{:S(2)}, u32[]{:S(2)}) %all-to-all-start) | async-done | bytes 1048608 | tf_op jit(solution)/shard_map/all_to_all | solution.py:22
  50.0 4.3 %convolution_convert_fusion.2 = bf16[1024,2048]{1,0:T(8,128)(2,1)} fusion(bf16[256,2048]{0,1:T(8,128)(2,1)S(1)} %bitcast.92, bf16[256,1024]{1,0:T(8,128)(2,1)} %convert_reduce_fusion.1), kind=kOutput, calls=%fused_computation.4 | convolution fusion | flops 1075838976 | bytes 5767168 | tf_op jit(solution)/shard_map/dot_general | solution.py:115
  54.4 5.1 %all-to-all-start.1 = ((bf16[8,128,2048]{2,1,0:T(8,128)(2,1)}), bf16[8,128,2048]{2,1,0:T(8,128)(2,1)}, u32[]{:S(2)}, u32[]{:S(2)}) async-start(bf16[8,128,2048]{2,1,0:T(8,128)(2,1)} %bitcast.83), calls=%async_computation.1 | async-start | bytes 8388608 | tf_op jit(solution)/shard_map/all_to_all | solution.py:157
  59.4 0.7 pad_maximum_fusion.1
  60.2 3.9 copy.35
  64.1 50.3 %all-to-all-done.1 = bf16[8,128,2048]{2,1,0:T(8,128)(2,1)} async-done(((bf16[8,128,2048]{2,1,0:T(8,128)(2,1)}), bf16[8,128,2048]{2,1,0:T(8,128)(2,1)}, u32[]{:S(2)}, u32[]{:S(2)}) %all-to-all-start.1) | async-done | bytes 4194336 | tf_op jit(solution)/shard_map/all_to_all | solution.py:157
  114.4 5.7 %fusion.32 = bf16[1024,512,1]{1,0,2:T(8,128)(2,1)S(1)} fusion(bf16[1024,2048]{1,0:T(8,128)(2,1)} %bitcast.8, bf16[1,2048,512]{2,1,0:T(8,128)(2,1)} %param.14), kind=kOutput, calls=%fused_computation.44 | convolution fusion | flops 2152202240 | bytes 7340032 | tf_op jit(solution)/shard_map/dot_general | solution.py:159
  120.1 2.4 fusion.49
  122.5 3.8 copy.32
  126.3 0.7 copy-done.10
  127.0 0.1 copy.34
  127.1 0.1 mul.138
  127.3 0.6 reduce-window.16
  127.9 0.2 slice_reduce_fusion
  128.2 0.1 copy.33
  128.4 0.1 eq.112
  128.5 0.3 convert_reduce_fusion
  128.8 79.0 %all-gather.2.cloned.1.call-done = bf16[512,2048]{1,0:T(8,128)(2,1)} async-done(((bf16[512,128]{1,0:T(8,128)(2,1)}), bf16[512,2048]{1,0:T(8,128)(2,1)}) %all-gather.2.cloned.1.call-update) | async-done | bytes 2097168 | tf_op jit(solution)/shard_map/all_gather | solution.py:56
  207.8 1.5 slice_convert_fusion
  209.3 4.4 %mul.140 = f32[256,2,2048]{2,1,0:T(2,128)} broadcast(f32[256,2048]{1,0:T(8,128)S(1)} %slice_convert_fusion), dimensions={0,2} | broadcast | bytes 6291456 | tf_op jit(solution)/shard_map/mul | solution.py:127
  213.7 6.1 %mul.141 = f32[512,2048]{1,0:T(8,128)} reshape(f32[256,2,2048]{2,1,0:T(2,128)} %mul.140) | data formatting | bytes 8388608 | tf_op jit(solution)/shard_map/mul | solution.py:127
  219.8 4.6 %convolution_convert_fusion.1 = bf16[1024,2048]{1,0:T(8,128)(2,1)} fusion(bf16[512,2048]{1,0:T(8,128)(2,1)} %all-gather.2.cloned.1.call-done, bf16[256,1024]{1,0:T(8,128)(2,1)S(1)} %convert_reduce_fusion), kind=kOutput, calls=%fused_computation.3 | convolution fusion | flops 1075838976 | bytes 5767168 | tf_op jit(solution)/shard_map/dot_general | solution.py:115
  224.4 4.6 %convolution_convert_fusion = bf16[1024,2048]{1,0:T(8,128)(2,1)} fusion(f32[512,2048]{1,0:T(8,128)S(1)} %copy-done.4, f32[512]{0:T(512)S(1)} %mul.138, s32[512]{0:T(512)S(1)} %eq.112), kind=kOutput, calls=%fused_computation.2 | convolution fusion | flops 2152202240 | bytes 8392704 | tf_op jit(solution)/shard_map/dot_general | solution.py:115
  228.9 8.3 %pad_maximum_fusion = bf16[8,256,2048]{2,1,0:T(8,128)(2,1)} fusion(bf16[8,128,2048]{2,1,0:T(8,128)(2,1)} %bitcast.93, bf16[8,128,2048]{2,1,0:T(8,128)(2,1)} %bitcast.84), kind=kLoop, calls=%fused_computation | loop fusion | flops 16777216 | bytes 16777216 | tf_op jit(solution)/shard_map/concatenate | solution.py:64
  237.2 5.7 %all-to-all-start.3 = ((bf16[8,256,2048]{2,1,0:T(8,128)(2,1)}), bf16[8,256,2048]{2,1,0:T(8,128)(2,1)}, u32[]{:S(2)}, u32[]{:S(2)}) async-start(bf16[8,256,2048]{2,1,0:T(8,128)(2,1)} %pad_maximum_fusion), calls=%async_computation.5 | async-start | bytes 16777216 | tf_op jit(solution)/shard_map/all_to_all | solution.py:67
  243.0 114.6 %all-to-all-done.3 = bf16[8,256,2048]{2,1,0:T(8,128)(2,1)} async-done(((bf16[8,256,2048]{2,1,0:T(8,128)(2,1)}), bf16[8,256,2048]{2,1,0:T(8,128)(2,1)}, u32[]{:S(2)}, u32[]{:S(2)}) %all-to-all-start.3) | async-done | bytes 8388640 | tf_op jit(solution)/shard_map/all_to_all | solution.py:67
  357.6 4.0 fusion.48
  361.6 1.7 constant_dynamic-slice_fusion.1
  363.3 4.3 %multiply_convert_fusion.2 = (bf16[1024,512]{1,0:T(8,128)(2,1)}, f32[1024,512]{1,0:T(8,128)}) fusion(bf16[1024,2048]{1,0:T(8,128)(2,1)S(1)} %bitcast.89, bf16[1,2048,512]{2,1,0:T(8,128)(2,1)S(1)} %copy-done), kind=kOutput, calls=%fused_computation.29 | convolution fusion | flops 2152202240 | bytes 9437184 | tf_op jit(solution)/shard_map/dot_general | solution.py:192
  367.7 1.6 constant_dynamic-slice_fusion
  369.2 0.5 collective-permute-start.3
  369.8 7.8 %fusion.11 = bf16[1024,512]{1,0:T(8,128)(2,1)} fusion(f32[1024,512]{1,0:T(8,128)} %get-tuple-element.6, bf16[1024,2048]{1,0:T(8,128)(2,1)} %bitcast.86, bf16[1,512,2048]{2,1,0:T(8,128)(2,1)} %param.21), kind=kOutput, calls=%fused_computation.19 | convolution fusion | flops 2157445120 | bytes 9437184 | tf_op jit(solution)/shard_map/dot_general | solution.py:194
  377.5 0.5 collective-permute-start.2
  378.1 3.4 fusion.20
  381.4 3.9 fusion.18
  385.3 3.9 fusion.26
  389.2 3.6 reduce-scatter.5.cloned.1.call-done
  392.8 1.8 convert_element_type.67
  394.6 4.8 %all-to-all-start.2 = ((bf16[8,128,128]{2,1,0:T(8,128)(2,1)}), bf16[8,128,128]{2,1,0:T(8,128)(2,1)S(1)}, u32[]{:S(2)}, u32[]{:S(2)}) async-start(bf16[8,128,128]{2,1,0:T(8,128)(2,1)} %bitcast.18), calls=%async_computation.4 | async-start | bytes 524288 | tf_op jit(solution)/shard_map/all_to_all | solution.py:163
  399.4 4.8 %fusion.27 = bf16[1,512,1024]{2,1,0:T(8,128)(2,1)} fusion(f32[512,1024]{1,0:T(8,128)} %fusion.18, bf16[1024,512]{1,0:T(8,128)(2,1)} %collective-permute-done.2, bf16[1024,1024]{1,0:T(8,128)(2,1)} %collective-permute-done.3), kind=kOutput, calls=%fused_computation.43 | convolution fusion | flops 1074790400 | bytes 6291456 | tf_op jit(solution)/shard_map/dot_general | solution.py:121
  404.2 0.2 all-to-all-done.2
  404.4 1.1 fusion.38
  (48 shorter events, 0.5 us)
Async XLA Ops:
  8.0 355.4 %copy-start = (bf16[1,2048,512]{2,1,0:T(8,128)(2,1)S(1)}, bf16[1,2048,512]{2,1,0:T(8,128)(2,1)}, u32[]{:S(2)}) copy-start(bf16[1,2048,512]{2,1,0:T(8,128)(2,1)} %param.20) | copy-start | bytes 6291460
  8.0 13.4 %copy-start.8 = (s32[256,2]{0,1:T(2,128)S(1)}, s32[256,2]{0,1:T(2,128)}, u32[]{:S(2)}) copy-start(s32[256,2]{0,1:T(2,128)} %param.12) | copy-start | bytes 6148
  10.2 39.8 %all-to-all-start = ((bf16[16,256,128]{1,2,0:T(8,128)(2,1)}), bf16[16,256,128]{1,2,0:T(8,128)(2,1)S(1)}, u32[]{:S(2)}, u32[]{:S(2)}) async-start(bf16[16,256,128]{1,2,0:T(8,128)(2,1)} %broadcast_in_dim.6), calls=%async_computation | async-start | bytes 2097152 | tf_op jit(solution)/shard_map/all_to_all | solution.py:22
  54.4 5.1 %copy-start.6 = (bf16[256,128]{1,0:T(8,128)(2,1)S(1)}, bf16[256,128]{1,0:T(8,128)(2,1)}, u32[]{:S(2)}) copy-start(bf16[256,128]{1,0:T(8,128)(2,1)} %param.19) | copy-start | bytes 196612
  54.4 5.1 %copy-start.7 = (bf16[256,128]{1,0:T(8,128)(2,1)S(1)}, bf16[256,128]{1,0:T(8,128)(2,1)}, u32[]{:S(2)}) copy-start(bf16[256,128]{1,0:T(8,128)(2,1)} %param.16) | copy-start | bytes 196612
  54.4 60.0 %all-to-all-start.1 = ((bf16[8,128,2048]{2,1,0:T(8,128)(2,1)}), bf16[8,128,2048]{2,1,0:T(8,128)(2,1)}, u32[]{:S(2)}, u32[]{:S(2)}) async-start(bf16[8,128,2048]{2,1,0:T(8,128)(2,1)} %bitcast.83), calls=%async_computation.1 | async-start | bytes 8388608 | tf_op jit(solution)/shard_map/all_to_all | solution.py:157
  59.4 148.4 %all-gather.2.cloned.1.call-start = ((), (), s32[]{:S(2)}) async-start(), calls=%async_computation.8 | async-start | bytes 2228224 | tf_op jit(solution)/shard_map/all_gather | solution.py:56
  60.1 309.6 %reduce-scatter.3.cloned.1.call-start = ((), (), s32[]{:S(2)}) async-start(), calls=%async_computation.6 | async-start | bytes 9437184 | tf_op jit(solution)/shard_map/reduce_scatter | solution.py:35
  114.4 5.7 %copy-start.5 = (bf16[2048,512]{1,0:T(8,128)(2,1)S(1)}, bf16[2048,512]{1,0:T(8,128)(2,1)}, u32[]{:S(2)}) copy-start(bf16[2048,512]{1,0:T(8,128)(2,1)} %copy.35) | copy-start | bytes 6291460
  126.3 0.7 copy-start.10
  126.3 1.0 copy-start.9
  219.8 4.6 %copy-start.4 = (f32[512,2048]{1,0:T(8,128)S(1)}, f32[512,2048]{1,0:T(8,128)}, u32[]{:S(2)}) copy-start(f32[512,2048]{1,0:T(8,128)} %mul.141) | copy-start | bytes 12582916
  237.2 120.4 %all-to-all-start.3 = ((bf16[8,256,2048]{2,1,0:T(8,128)(2,1)}), bf16[8,256,2048]{2,1,0:T(8,128)(2,1)}, u32[]{:S(2)}, u32[]{:S(2)}) async-start(bf16[8,256,2048]{2,1,0:T(8,128)(2,1)} %pad_maximum_fusion), calls=%async_computation.5 | async-start | bytes 16777216 | tf_op jit(solution)/shard_map/all_to_all | solution.py:67
  243.0 149.8 %reduce-scatter.5.cloned.1.call-start = ((), (), s32[]{:S(2)}) async-start(), calls=%async_computation.7 | async-start | bytes 1572864 | tf_op jit(solution)/shard_map/reduce_scatter | solution.py:35
  361.6 6.1 %copy-start.3 = (bf16[8,128,2048]{2,1,0:T(8,128)(2,1)}, bf16[8,128,2048]{2,1,0:T(8,128)(2,1)S(1)}, u32[]{:S(2)}) copy-start(bf16[8,128,2048]{2,1,0:T(8,128)(2,1)S(1)} %get-tuple-element.4) | copy-start | bytes 12582916
  361.6 6.0 %copy-start.1 = (bf16[8,128,2048]{2,1,0:T(8,128)(2,1)}, bf16[8,128,2048]{2,1,0:T(8,128)(2,1)S(1)}, u32[]{:S(2)}) copy-start(bf16[8,128,2048]{2,1,0:T(8,128)(2,1)S(1)} %get-tuple-element.3) | copy-start | bytes 12582916
  363.3 22.0 %collective-permute-start = (bf16[1024,1024]{1,0:T(8,128)(2,1)}, bf16[1024,1024]{1,0:T(8,128)(2,1)}, u32[]{:S(2)}, u32[]{:S(2)}) collective-permute-start(bf16[1024,1024]{1,0:T(8,128)(2,1)} %constant_dynamic-slice_fusion.1), channel_id=1, source_target_pairs={{0,1},{1,0},{2,3},{3,2},{4,5},{5,4},{6,7},{7,6},{8,9},{9,8},{10,11... | collective-permute-start | bytes 6291464 | tf_op jit(solution)/shard_map/ppermute | solution.py:77
  369.2 30.2 %collective-permute-start.3 = (bf16[1024,1024]{1,0:T(8,128)(2,1)}, bf16[1024,1024]{1,0:T(8,128)(2,1)}, u32[]{:S(2)}, u32[]{:S(2)}) collective-permute-start(bf16[1024,1024]{1,0:T(8,128)(2,1)} %constant_dynamic-slice_fusion), channel_id=1, source_target_pairs={{0,1},{1,0},{2,3},{3,2},{4,5},{5,4},{6,7},{7,6},{8,9},{9,8},{10,11... | collective-permute-start | bytes 6291464 | tf_op jit(solution)/shard_map/ppermute | solution.py:77
  377.5 7.8 %collective-permute-start.1 = (bf16[1024,512]{1,0:T(8,128)(2,1)}, bf16[1024,512]{1,0:T(8,128)(2,1)S(1)}, u32[]{:S(2)}, u32[]{:S(2)}) collective-permute-start(bf16[1024,512]{1,0:T(8,128)(2,1)} %fusion.11), channel_id=1, source_target_pairs={{0,1},{1,0},{2,3},{3,2},{4,5},{5,4},{6,7},{7,6},{8,9},{9,8},{10,11... | collective-permute-start | bytes 3145736 | tf_op jit(solution)/shard_map/ppermute | solution.py:77
  377.5 3.9 copy-start.2
  377.5 21.8 %collective-permute-start.2 = (bf16[1024,512]{1,0:T(8,128)(2,1)}, bf16[1024,512]{1,0:T(8,128)(2,1)}, u32[]{:S(2)}, u32[]{:S(2)}) collective-permute-start(bf16[1024,512]{1,0:T(8,128)(2,1)} %get-tuple-element.5), channel_id=1, source_target_pairs={{0,1},{1,0},{2,3},{3,2},{4,5},{5,4},{6,7},{7,6},{8,9},{9,8},{10,11... | collective-permute-start | bytes 3145736 | tf_op jit(solution)/shard_map/ppermute | solution.py:77
  394.6 9.8 %all-to-all-start.2 = ((bf16[8,128,128]{2,1,0:T(8,128)(2,1)}), bf16[8,128,128]{2,1,0:T(8,128)(2,1)S(1)}, u32[]{:S(2)}, u32[]{:S(2)}) async-start(bf16[8,128,128]{2,1,0:T(8,128)(2,1)} %bitcast.18), calls=%async_computation.4 | async-start | bytes 524288 | tf_op jit(solution)/shard_map/all_to_all | solution.py:163
  399.4 5.0 %copy-start.11 = (f32[256,2]{0,1:T(2,128)S(1)}, f32[256,2]{0,1:T(2,128)}, u32[]{:S(2)}) copy-start(f32[256,2]{0,1:T(2,128)} %param.13) | copy-start | bytes 6148
Sparse Core Ops, SparseCore 0:
  63.3 144.5 all-gather.1
Sparse Core Ops, SparseCore 1:
  126.4 101.6 reduce-scatter.2
  369.9 22.9 reduce-scatter.4
where the time goes:
time: 415 us; the launch traced here: 413 us
  waiting for transfers between devices  274 us (66%)
  matrix products  50.7 us (12%)
  local copies, waits for them, and re-layouts  29.3 us (7%)
  starting transfers between devices  27.9 us (7%)
  between operations  15.7 us (4%)
  other arithmetic  15 us (4%)
    all_to_all x1, waiting for transfers between devices, in_one_piece(): lax.all_to_all(both, axis, split_axis=split_dim, concat_axis=concat_dim,...  115 us
    all_gather x1, waiting for transfers between devices, sent_together(): lax.all_gather(both, axis, axis=dim, tiled=True)  79 us
    all_to_all x1, waiting for transfers between devices, on_device(): lax.all_to_all(sent, 'expert', split_axis=0, concat_axis=0, tiled=True)  50.3 us
    all_to_all x1, waiting for transfers between devices, sent_to_all(): return lax.all_to_all(copies, axis, split_axis=0, concat_axis=0, tiled=True)  26.6 us
    dot_general x4, matrix products, over_rows(): lax.dot_general(left, right, (((0,), (0,)), ((), ())), preferred_element_...  15.9 us
    dot_general x3, matrix products, to_slots(): lax.dot_general(matrix, rows, (((0,), (0,)), ((), ())), preferred_element...  13.5 us
    all_to_all x1, starting transfers between devices, sent_to_all(): return lax.all_to_all(copies, axis, split_axis=0, concat_axis=0, tiled=True)  11.2 us
    mul x3, local copies, waits for them, and re-layouts, scale_rows(): scaled = gates[:, :, None] * rows[:, None, :].astype(jnp.float32)  10.6 us
  transfers between devices with their start and end apart: 11, of which 6 were waited for; matrix products, arithmetic and copies ran while one was open for 21% of the time, Pallas kernels for 0%

commit v1 on v0

--- a/solution.py
+++ b/solution.py
@@ -148,47 +148,52 @@
     total = experts * capacity
     w_up = up_real[0]
     w_down = down_real[0]
+    wf_up = up_fake[0]
+    wf_down = down_fake[0]
     real_pos = slot_index(routes_real, experts, capacity)
     real_pick = spread_matrix(real_pos, total)
-    whole = gather_directly(x_real, TENSOR, 1)
-    sent = (
-        to_slots(real_pick, whole).astype(jnp.bfloat16).reshape(experts, capacity, whole.shape[1])
-    )
+    whole = lax.all_gather(x_real, TENSOR, axis=1, tiled=True)
+
+    fake_pos = slot_index(routes_fake, experts, capacity)
+    fake_pick = spread_matrix(fake_pos, total)
+    fake_flat = pick_matrix(fake_pos, total)
+    part = x_fake.shape[1]
+    sent_x = to_slots(fake_pick, x_fake).astype(jnp.bfloat16).reshape(experts, capacity, part)
+    sent_d = (
+        to_slots(fake_flat, scale_rows(gates_fake, cotangent))
+        .astype(jnp.bfloat16)
+        .reshape(experts, capacity, part)
+    )
+    got_x, got_d = in_one_piece((sent_x, sent_d), "expert", 0, 0, 1)
+    both = jnp.concatenate((got_x.reshape(total, part), got_d.reshape(total, part)), axis=0)
+    whole, both = lax.optimization_barrier((whole, both))
+    both = lax.all_gather(both, TENSOR, axis=1, tiled=True)
+    rows_x, rows_d = both[:total], both[total:]
+
+    width = whole.shape[1]
+    sent = to_slots(real_pick, whole).astype(jnp.bfloat16).reshape(experts, capacity, width)
     arrived = lax.all_to_all(sent, "expert", split_axis=0, concat_axis=0, tiled=True)
-    rows = arrived.reshape(total, arrived.shape[2])
+    rows = arrived.reshape(total, width)
     pre_real = jnp.dot(rows, w_up, preferred_element_type=jnp.float32)
     hidden = gelu_tanh(pre_real).astype(jnp.bfloat16)
-    partial_out = jnp.dot(hidden, w_down, preferred_element_type=jnp.float32)
-    summed = sum_by_axis(partial_out, TENSOR, (1, 0), 1).astype(jnp.bfloat16)
+    partial_out = jnp.dot(hidden, w_down, preferred_element_type=jnp.float32).astype(jnp.bfloat16)
     returned = lax.all_to_all(
-        summed.reshape(experts, capacity, summed.shape[1]),
+        partial_out.reshape(experts, capacity, width),
         "expert",
         split_axis=0,
         concat_axis=0,
         tiled=True,
-    )
-    returned = returned.reshape(total, returned.shape[2])
-    real_flat = pick_matrix(real_pos, total)
-    picked = jnp.dot(real_flat, returned, preferred_element_type=jnp.float32).reshape(
-        tokens, top, returned.shape[1]
-    )
-    real_out = jnp.sum(gates_real[:, :, None] * picked, axis=1).astype(jnp.bfloat16)
-    fake_pos = slot_index(routes_fake, experts, capacity)
-    fake_pick = spread_matrix(fake_pos, total)
-    fake_flat = pick_matrix(fake_pos, total)
-    whole_x, whole_c = sent_together((x_fake, cotangent), TENSOR, 1, 0)
-    width = whole_x.shape[1]
-    sent_x = to_slots(fake_pick, whole_x).astype(jnp.bfloat16).reshape(experts, capacity, width)
-    sent_d = (
-        to_slots(fake_flat, scale_rows(gates_fake, whole_c))
-        .astype(jnp.bfloat16)
-        .reshape(experts, capacity, width)
-    )
-    got_x, got_d = in_one_piece((sent_x, sent_d), "expert", 0, 0, 1)
-    rows_x = got_x.reshape(total, width)
-    rows_d = got_d.reshape(total, width)
-    wf_up = up_fake[0]
-    wf_down = down_fake[0]
+    ).reshape(total, width)
+    columns = jnp.arange(total, dtype=jnp.int32)
+    match = (real_pos[:, :, None] == columns[None, None, :]).astype(jnp.float32)
+    weights = jnp.sum(match * gates_real[:, :, None], axis=1)
+    high = weights.astype(jnp.bfloat16)
+    low = (weights - high.astype(jnp.float32)).astype(jnp.bfloat16)
+    combined = jnp.dot(high, returned, preferred_element_type=jnp.float32) + jnp.dot(
+        low, returned, preferred_element_type=jnp.float32
+    )
+    real_out = sum_by_axis(combined, TENSOR, (1, 0), 1).astype(jnp.bfloat16)
+
     pre_fake = jnp.dot(rows_x, wf_up, preferred_element_type=jnp.float32)
     act = gelu_tanh(pre_fake).astype(jnp.bfloat16)
     back_act = lax.dot_general(

time: 415 us -> 433 us (1.043)
  blocking collectives: 0 us -> 95.4 us
  starting transfers between devices: 27.9 us -> 7.14 us
  waiting for transfers between devices: 274 us -> 254 us
  matrix products: 50.7 us -> 36 us
  local copies, waits for them, and re-layouts: 29.3 us -> 17 us
  other arithmetic: 15 us -> 8.19 us
    all_gather x1 -> x2, waiting for transfers between devices: 79 us -> 208 us  [the longest x1 149 us: on_device(): both = lax.all_gather(both, TENSOR, axis=1, tiled=True)]
    all_to_all x1, waiting for transfers between devices: 115 us -> 4.92 us  [in_one_piece(): lax.all_to_all(both, axis, split_axis=split_dim, concat_axis=concat_dim,...]
    all_to_all x0 -> x2, blocking collectives: none -> 95.4 us  [the longest x1 48 us: on_device(): lax.all_to_all(sent, 'expert', split_axis=0, concat_axis=0, tiled=True)]
    all_to_all x3 -> x0, waiting for transfers between devices: 77 us -> none  [the longest x1 50.3 us: on_device(): lax.all_to_all(sent, 'expert', split_axis=0, concat_axis=0, tiled=True)]
    reduce_scatter x2, waiting for transfers between devices: 3.62 us -> 39.5 us  [reduced_to_own(): pieces = lax.psum_scatter(pieces, axes[k], scatter_dimension=0, tiled=True)]
    all_to_all x3 -> x0, starting transfers between devices: 21.1 us -> none  [the longest x1 11.2 us: sent_to_all(): return lax.all_to_all(copies, axis, split_axis=0, concat_axis=0, tiled=True)]
    dot_general x3, matrix products: 13.5 us -> 3.9 us  [to_slots(): lax.dot_general(matrix, rows, (((0,), (0,)), ((), ())), preferred_element...]
    mul x3 -> x2, local copies, waits for them, and re-layouts: 10.6 us -> 1.06 us  [scale_rows(): scaled = gates[:, :, None] * rows[:, None, :].astype(jnp.float32)]
  transfers between devices with their start and end apart: 11 -> 9, of which waited for: 6 -> 4; matrix products, arithmetic and copies ran while one was open for 21% -> 8% of each run, Pallas kernels for 0% -> 0%
where the time goes in v1:
time: 433 us; the launch traced here: 432 us
  waiting for transfers between devices  254 us (59%)
  blocking collectives  95.4 us (22%)
  matrix products  36 us (8%)
  local copies, waits for them, and re-layouts  17 us (4%)
  between operations  14 us (3%)
  other arithmetic  8.19 us (2%)
  starting transfers between devices  7.14 us (2%)
    all_gather x1, waiting for transfers between devices, on_device(): both = lax.all_gather(both, TENSOR, axis=1, tiled=True)  149 us
    all_gather x1, waiting for transfers between devices, on_device(): whole = lax.all_gather(x_real, TENSOR, axis=1, tiled=True)  59.5 us
    all_to_all x1, blocking collectives, on_device(): lax.all_to_all(sent, 'expert', split_axis=0, concat_axis=0, tiled=True)  48 us
    all_to_all x1, blocking collectives, on_device(): lax.all_to_all(partial_out.reshape(experts, capacity, width), 'expert', s...  47.4 us
    reduce_scatter x2, waiting for transfers between devices, reduced_to_own(): pieces = lax.psum_scatter(pieces, axes[k], scatter_dimension=0, tiled=True)  39.5 us
    dot_general x4, matrix products, over_rows(): lax.dot_general(left, right, (((0,), (0,)), ((), ())), preferred_element_...  12.8 us
    dot_general x1, matrix products, on_device(): jnp.dot(hidden, w_down, preferred_element_type=jnp.float32)  9.63 us
  transfers between devices with their start and end apart: 9, of which 4 were waited for; matrix products, arithmetic and copies ran while one was open for 8% of the time, Pallas kernels for 0%

profile of v1, /device:TPU:6, one launch (start us, length us, event | category | flops | bytes accessed | tf_op | source)
XLA Modules:
  0.0 431.7 jit_solution(8961847231231430238)
XLA Ops:
  7.2 0.7 all-gather.3.cloned.1.call-update
  7.9 0.7 convert_reduce_fusion.2
  8.6 0.6 reduce-window.16
  9.2 0.2 slice_reduce_fusion
  9.5 0.7 select_reduce_fusion.1
  10.2 0.7 multiply_add_fusion.2
  10.9 0.1 copy.30
  11.1 0.1 eq.86
  11.2 0.8 copy.31
  12.0 0.1 mul.132
  12.2 0.9 mul.134
  13.1 0.9 fusion.31
  14.0 0.3 convert_reduce_fusion
  14.3 0.3 convolution_convert_fusion.2
  14.6 0.8 pad_maximum_fusion
  15.5 6.2 %all-to-all-start = ((bf16[8,256,128]{2,1,0:T(8,128)(2,1)}), bf16[8,256,128]{2,1,0:T(8,128)(2,1)}, u32[]{:S(2)}, u32[]{:S(2)}) async-start(bf16[8,256,128]{2,1,0:T(8,128)(2,1)} %pad_maximum_fusion), calls=%async_computation | async-start | bytes 1048576 | tf_op jit(solution)/shard_map/all_to_all | solution.py:67
  21.7 0.6 reduce-window.14
  22.3 0.2 slice_reduce_fusion.1
  22.7 1.2 select_reduce_fusion
  23.9 4.9 %all-to-all-done = bf16[8,256,128]{2,1,0:T(8,128)(2,1)} async-done(((bf16[8,256,128]{2,1,0:T(8,128)(2,1)}), bf16[8,256,128]{2,1,0:T(8,128)(2,1)}, u32[]{:S(2)}, u32[]{:S(2)}) %all-to-all-start) | async-done | bytes 524320 | tf_op jit(solution)/shard_map/all_to_all | solution.py:67
  28.8 1.1 fusion.50
  29.9 0.8 pad_maximum_fusion.1
  30.7 59.5 %all-gather.3.cloned.1.call-done = bf16[256,2048]{1,0:T(8,128)(2,1)} async-done(((bf16[256,128]{1,0:T(8,128)(2,1)}), bf16[256,2048]{1,0:T(8,128)(2,1)}) %all-gather.3.cloned.1.call-update) | async-done | bytes 1048592 | tf_op jit(solution)/shard_map/all_gather | solution.py:155
  90.2 2.7 convolution_convert_fusion.1
  92.9 48.0 %all_to_all.15 = bf16[8,128,2048]{2,1,0:T(8,128)(2,1)} all-to-all(bf16[8,128,2048]{2,1,0:T(8,128)(2,1)S(1)} %bitcast.72), channel_id=1, replica_groups=mesh['expert'=8,'tensor_0'=2,'tensor_1'=8,'dp'=2] {'expert'}, dimensions={0} | all-to-all | bytes 8388608 | tf_op jit(solution)/shard_map/all_to_all | solution.py:175
  141.0 9.6 %convolution_convert_fusion = bf16[1024,2048]{1,0:T(8,128)(2,1)} fusion(bf16[1,512,2048]{2,1,0:T(8,128)(2,1)S(1)} %copy-done, bf16[1024,2048]{1,0:T(8,128)(2,1)} %bitcast.77, bf16[1,2048,512]{2,1,0:T(8,128)(2,1)} %param.14), kind=kOutput, calls=%fused_computation | convolution fusion | flops 4301783040 | bytes 12582912 | tf_op jit(solution)/shard_map/dot_general | solution.py:179
  150.6 47.4 %all_to_all.16 = bf16[8,128,2048]{2,1,0:T(8,128)(2,1)S(1)} all-to-all(bf16[8,128,2048]{2,1,0:T(8,128)(2,1)} %bitcast.78), channel_id=1, replica_groups=mesh['expert'=8,'tensor_0'=2,'tensor_1'=8,'dp'=2] {'expert'}, dimensions={0} | all-to-all | bytes 8388608 | tf_op jit(solution)/shard_map/all_to_all | solution.py:180
  198.0 1.3 fusion.38
  199.2 1.3 fusion.24
  200.6 0.4 copy.33
  201.0 2.0 copy.32
  203.1 0.7 all-gather.5.cloned.1.call-update
  203.8 39.5 %reduce-scatter.3.cloned.1.call-done = f32[2,256,128]{2,1,0:T(8,128)} async-done(((f32[16,256,128]{2,1,0:T(8,128)}), f32[2,256,128]{2,1,0:T(8,128)}) %reduce-scatter.3.cloned.1.call-update) | async-done | bytes 262160 | tf_op jit(solution)/shard_map/reduce_scatter | solution.py:35
  243.4 148.7 %all-gather.5.cloned.1.call-done = bf16[2048,2048]{1,0:T(8,128)(2,1)} async-done(((bf16[2048,128]{1,0:T(8,128)(2,1)}), bf16[2048,2048]{1,0:T(8,128)(2,1)}) %all-gather.5.cloned.1.call-update) | async-done | bytes 8388624 | tf_op jit(solution)/shard_map/all_gather | solution.py:170
  392.1 4.1 fusion.49
  396.2 0.2 constant_dynamic-slice_fusion.1
  396.5 0.3 collective-permute-start
  396.8 1.6 copy-done.2
  398.3 1.6 constant_dynamic-slice_fusion
  399.9 3.3 copy-done.5
  403.3 2.7 multiply_convert_fusion
  406.0 4.3 fusion.11
  410.3 1.5 convert_bitcast_fusion
  411.8 0.5 collective-permute-start.2
  412.3 3.4 fusion.21
  415.7 1.3 fusion.19
  417.1 4.3 fusion.25
  421.3 3.9 fusion.26
  (42 shorter events, 0.5 us)
Async XLA Ops:
  7.2 133.8 %copy-start = (bf16[1,512,2048]{2,1,0:T(8,128)(2,1)S(1)}, bf16[1,512,2048]{2,1,0:T(8,128)(2,1)}, u32[]{:S(2)}) copy-start(bf16[1,512,2048]{2,1,0:T(8,128)(2,1)} %param.15) | copy-start | bytes 6291460
  7.2 7.1 %copy-start.6 = (bf16[256,128]{1,0:T(8,128)(2,1)S(1)}, bf16[256,128]{1,0:T(8,128)(2,1)}, u32[]{:S(2)}) copy-start(bf16[256,128]{1,0:T(8,128)(2,1)} %param.16) | copy-start | bytes 196612
  7.2 83.1 %all-gather.3.cloned.1.call-start = ((), (), s32[]{:S(2)}) async-start(), calls=%async_computation.5 | async-start | bytes 1114112 | tf_op jit(solution)/shard_map/all_gather | solution.py:155
  13.1 8.6 %copy-start.7 = (s32[256,2]{0,1:T(2,128)S(1)}, s32[256,2]{0,1:T(2,128)}, u32[]{:S(2)}) copy-start(s32[256,2]{0,1:T(2,128)} %param.12) | copy-start | bytes 6148
  13.1 9.6 %copy-start.8 = (f32[256,2]{0,1:T(2,128)S(1)}, f32[256,2]{0,1:T(2,128)}, u32[]{:S(2)}) copy-start(f32[256,2]{0,1:T(2,128)} %param.13) | copy-start | bytes 6148
  15.5 13.4 %all-to-all-start = ((bf16[8,256,128]{2,1,0:T(8,128)(2,1)}), bf16[8,256,128]{2,1,0:T(8,128)(2,1)}, u32[]{:S(2)}, u32[]{:S(2)}) async-start(bf16[8,256,128]{2,1,0:T(8,128)(2,1)} %pad_maximum_fusion), calls=%async_computation | async-start | bytes 1048576 | tf_op jit(solution)/shard_map/all_to_all | solution.py:67
  21.7 221.7 %reduce-scatter.3.cloned.1.call-start = ((), (), s32[]{:S(2)}) async-start(), calls=%async_computation.6 | async-start | bytes 2359296 | tf_op jit(solution)/shard_map/reduce_scatter | solution.py:35
  203.0 189.0 %all-gather.5.cloned.1.call-start = ((), (), s32[]{:S(2)}) async-start(), calls=%async_computation.8 | async-start | bytes 8912896 | tf_op jit(solution)/shard_map/all_gather | solution.py:170
  203.8 206.5 %reduce-scatter.5.cloned.1.call-start = ((), (), s32[]{:S(2)}) async-start(), calls=%async_computation.7 | async-start | bytes 393216 | tf_op jit(solution)/shard_map/reduce_scatter | solution.py:35
  392.1 7.9 %copy-start.9 = (bf16[1,2048,512]{2,1,0:T(8,128)(2,1)S(1)}, bf16[1,2048,512]{2,1,0:T(8,128)(2,1)}, u32[]{:S(2)}) copy-start(bf16[1,2048,512]{2,1,0:T(8,128)(2,1)} %param.20) | copy-start | bytes 6291460
  396.2 2.1 copy-start.2
  396.2 9.8 %copy-start.4 = (bf16[1024,2048]{1,0:T(8,128)(2,1)}, bf16[1024,2048]{1,0:T(8,128)(2,1)S(1)}, u32[]{:S(2)}) copy-start(bf16[1024,2048]{1,0:T(8,128)(2,1)S(1)} %get-tuple-element.10) | copy-start | bytes 12582916
  396.2 7.0 %copy-start.5 = (bf16[2048,2048]{1,0:T(8,128)(2,1)S(1)}, bf16[2048,2048]{1,0:T(8,128)(2,1)}, u32[]{:S(2)}) copy-start(bf16[2048,2048]{1,0:T(8,128)(2,1)} %all-gather.5.cloned.1.call-done) | copy-start | bytes 25165828
  396.5 20.6 %collective-permute-start = (bf16[1024,1024]{1,0:T(8,128)(2,1)S(1)}, bf16[1024,1024]{1,0:T(8,128)(2,1)}, u32[]{:S(2)}, u32[]{:S(2)}) collective-permute-start(bf16[1024,1024]{1,0:T(8,128)(2,1)S(1)} %constant_dynamic-slice_fusion.1), channel_id=1, source_target_pairs={{0,1},{1,0},{2,3},{3,2},{4,5},{5,4},{6,7},{7,6},{8,9},{9,8},{10,11... | collective-permute-start | bytes 6291464 | tf_op jit(solution)/shard_map/ppermute | solution.py:77
  399.9 6.1 %copy-start.10 = (bf16[1,512,2048]{2,1,0:T(8,128)(2,1)S(1)}, bf16[1,512,2048]{2,1,0:T(8,128)(2,1)}, u32[]{:S(2)}) copy-start(bf16[1,512,2048]{2,1,0:T(8,128)(2,1)} %param.21) | copy-start | bytes 6291460
  399.9 21.4 %collective-permute-start.3 = (bf16[1024,1024]{1,0:T(8,128)(2,1)}, bf16[1024,1024]{1,0:T(8,128)(2,1)}, u32[]{:S(2)}, u32[]{:S(2)}) collective-permute-start(bf16[1024,1024]{1,0:T(8,128)(2,1)} %constant_dynamic-slice_fusion), channel_id=1, source_target_pairs={{0,1},{1,0},{2,3},{3,2},{4,5},{5,4},{6,7},{7,6},{8,9},{9,8},{10,11... | collective-permute-start | bytes 6291464 | tf_op jit(solution)/shard_map/ppermute | solution.py:77
  410.3 6.8 %collective-permute-start.1 = (bf16[1024,512]{1,0:T(8,128)(2,1)}, bf16[1024,512]{1,0:T(8,128)(2,1)}, u32[]{:S(2)}, u32[]{:S(2)}) collective-permute-start(bf16[1024,512]{1,0:T(8,128)(2,1)} %fusion.11), channel_id=1, source_target_pairs={{0,1},{1,0},{2,3},{3,2},{4,5},{5,4},{6,7},{7,6},{8,9},{9,8},{10,11... | collective-permute-start | bytes 3145736 | tf_op jit(solution)/shard_map/ppermute | solution.py:77
  411.8 3.9 copy-start.3
  411.8 9.5 %collective-permute-start.2 = (bf16[1024,512]{1,0:T(8,128)(2,1)S(1)}, bf16[1024,512]{1,0:T(8,128)(2,1)S(1)}, u32[]{:S(2)}, u32[]{:S(2)}) collective-permute-start(bf16[1024,512]{1,0:T(8,128)(2,1)S(1)} %get-tuple-element.13), channel_id=1, source_target_pairs={{0,1},{1,0},{2,3},{3,2},{4,5},{5,4},{6,7},{7,6},{8,9},{9,8},{10,11... | collective-permute-start | bytes 3145736 | tf_op jit(solution)/shard_map/ppermute | solution.py:77
  417.1 8.1 %copy-start.1 = (bf16[1,512,2048]{2,1,0:T(8,128)(2,1)S(1)}, bf16[1,512,2048]{2,1,0:T(8,128)(2,1)}, u32[]{:S(2)}) copy-start(bf16[1,512,2048]{2,1,0:T(8,128)(2,1)} %param.15) | copy-start | bytes 6291460
Sparse Core Ops, SparseCore 0:
  10.5 79.7 all-gather.2
  203.2 40.1 reduce-scatter.2
  246.4 145.5 all-gather.4
  394.4 14.5 reduce-scatter.4

commit v2 on v0

v2 whole, which is shorter than its diff:
```python
import functools

import jax
import jax.numpy as jnp
from jax import lax
from jax.experimental import pallas as pl
from jax.experimental.pallas import tpu as pltpu
from jax.sharding import PartitionSpec as P

MESH = pl.DeviceIdType.MESH
BF = jnp.bfloat16
F32 = jnp.float32

slope_const = 0.7978845608028654
cubic_coef = 0.044715


def gelu_tanh(value):
    return (
        0.5 * value * (1.0 + jnp.tanh(slope_const * (value + cubic_coef * value * value * value)))
    )


def gelu_both(value):
    square = value * value
    inner = jnp.tanh(slope_const * (value + cubic_coef * square * value))
    act = 0.5 * value * (1.0 + inner)
    slope = 0.5 * (1.0 + inner) + 0.5 * value * (1.0 - inner * inner) * slope_const * (
        1.0 + 3.0 * cubic_coef * square
    )
    return act, slope


def slot_index(routes, experts, capacity):
    labels = jnp.arange(experts, dtype=jnp.int32)
    hits = (routes[:, :, None] == labels[None, None, :]).astype(jnp.int32)
    per_token = jnp.sum(hits, axis=1)
    before = jnp.cumsum(per_token, axis=0) - per_token
    slots = jnp.sum(hits * before[:, None, :], axis=2)
    return routes * capacity + slots


def spread_matrix(position, total):
    columns = jnp.arange(total, dtype=jnp.int32)
    match = (position[:, :, None] == columns[None, None, :]).astype(jnp.float32)
    return jnp.sum(match, axis=1).astype(BF)


def pick_matrix(position, total):
    columns = jnp.arange(total, dtype=jnp.int32)
    flat = position.reshape(-1)
    return (flat[:, None] == columns[None, :]).astype(BF)


def over_rows(left, right):
    return lax.dot_general(left, right, (((0,), (0,)), ((), ())), preferred_element_type=F32)


def scale_rows(gates, rows):
    scaled = gates[:, :, None] * rows[:, None, :].astype(F32)
    return scaled.astype(BF).reshape(-1, rows.shape[1])


def kernel(
    sizes,
    xr_ref,
    spread_ref,
    high_ref,
    low_ref,
    sx_ref,
    sd_ref,
    wru_hbm,
    wrd_hbm,
    wfu_hbm,
    wfd_hbm,
    out_ref,
    gu_ref,
    gd_ref,
    wru,
    wrd,
    wfu,
    wfd,
    xt,
    sent,
    rows,
    po,
    ret,
    xf,
    df,
    px,
    pd,
    act,
    dpre,
    pact,
    pdpre,
    slope,
    hidden,
    cs,
    rs,
    w_sem,
    loc_sem,
    xt_send,
    xt_yh,
    xt_recv,
    fd_send,
    fd_recv,
    f_send,
    f_yh,
    f_recv,
    rd_send,
    rd_recv,
    rt_send,
    rt_recv,
    rs_send,
    rs_recv,
    dp_send,
    dp_recv,
):
    ne, nz, cap = sizes
    e = lax.axis_index("expert")
    t = lax.axis_index("tensor")
    dp = lax.axis_index("dp")
    yh = t // nz
    z = t % nz
    oy = 1 - yh
    wide = nz * 128
    total = ne * cap

    def near(step):
        return (z + step + nz) % nz

    def cols(zz, sub):
        y = yh if sub == 0 else oy
        return pl.ds(pl.multiple_of(y * wide + zz * 128, 128), 128)

    def block(expert):
        return pl.ds(pl.multiple_of(expert * cap, cap), cap)

    def remote(src, dst, send, recv, where):
        pltpu.make_async_remote_copy(
            src_ref=src, dst_ref=dst, send_sem=send, recv_sem=recv, device_id=where, device_id_type=MESH
        ).start()

    def local(src, dst, sem):
        pltpu.make_async_copy(src, dst, sem).start()

    def landed(ref, sem):
        pltpu.make_async_copy(ref, ref, sem).wait()

    here = (e, t, dp)
    other = (e, oy * nz + z, dp)
    mate = (e, t, 1 - dp)
    sides = ((e, yh * nz + near(1), dp), (e, yh * nz + near(-1), dp))

    for i, (src, dst) in enumerate(((wru_hbm, wru), (wrd_hbm, wrd), (wfu_hbm, wfu), (wfd_hbm, wfd))):
        local(src, dst, w_sem.at[i])
    local(xr_ref, xt.at[:, cols(z, 0)], loc_sem)

    barrier = pltpu.get_barrier_semaphore()

    def greet_expert(k, _):
        pl.semaphore_signal(
            barrier, inc=1, device_id=((e + k) % ne, t, dp), device_id_type=MESH
        )
        return 0

    def greet_tensor(k, _):
        pl.semaphore_signal(
            barrier, inc=1, device_id=(e, (t + k) % (2 * nz), dp), device_id_type=MESH
        )
        return 0

    lax.fori_loop(1, ne, greet_expert, 0)
    lax.fori_loop(1, 2 * nz, greet_tensor, 0)
    pl.semaphore_signal(barrier, inc=1, device_id=mate, device_id_type=MESH)
    pl.semaphore_wait(barrier, ne + 2 * nz - 1)

    def ring_send(ref, zz, sub, way, dist, send, recv):
        remote(
            ref.at[:, cols(zz, sub)],
            ref.at[:, cols(zz, sub)],
            send,
            recv.at[way, dist - 1, sub],
            sides[way],
        )

    def ring_take(ref, dist, sub, send, recv):
        for way in (0, 1):
            if dist == nz // 2 and way != sub:
                continue
            zz = near(-dist if way == 0 else dist)
            landed(ref.at[:, cols(zz, sub)], recv.at[way, dist - 1, sub])
            if dist < nz // 2 - 1 or (dist == nz // 2 - 1 and way == sub):
                ring_send(ref, zz, sub, way, dist + 1, send, recv)

    local_x = pltpu.make_async_copy(xr_ref, xt.at[:, cols(z, 0)], loc_sem)
    local_x.wait()
    for way in (0, 1):
        ring_send(xt, z, 0, way, 1, xt_send, xt_recv)
    remote(xt.at[:, cols(z, 0)], xt.at[:, cols(z, 0)], xt_send, xt_yh, other)

    for i, (src, dst) in enumerate(((sx_ref, xf), (sd_ref, df))):

        def give(k, _, i=i, src=src, dst=dst):
            to = (e + k) % ne
            remote(
                src.at[block(to), :],
                dst.at[block(e), cols(z, 0)],
                fd_send.at[i],
                fd_recv.at[i],
                (to, t, dp),
            )
            return 0

        lax.fori_loop(1, ne, give, 0)
        local(src.at[block(e), :], dst.at[block(e), cols(z, 0)], fd_recv.at[i])

    def slot(zz, sub):
        sent[:, cols(zz, sub)] = jnp.dot(
            spread_ref[...], xt[:, cols(zz, sub)], preferred_element_type=F32
        ).astype(BF)

    def dispatch(zz, sub):
        def give(k, _):
            to = (e + k) % ne
            remote(
                sent.at[block(to), cols(zz, sub)],
                rows.at[block(e), cols(zz, sub)],
                rd_send,
                rd_recv,
                (to, t, dp),
            )
            return 0

        lax.fori_loop(1, ne, give, 0)

    def real_step(dist, sub):
        ring_take(xt, dist, sub, xt_send, xt_recv)
        if dist == nz // 2:
            slot(near(dist), sub)
            dispatch(near(dist), sub)
        else:
            slot(near(-dist), sub)
            slot(near(dist), sub)
            dispatch(near(-dist), sub)
            dispatch(near(dist), sub)

    slot(z, 0)
    landed(xt.at[:, cols(z, 1)], xt_yh)
    for way in (0, 1):
        ring_send(xt, z, 1, way, 1, xt_send, xt_recv)
    slot(z, 1)
    dispatch(z, 0)
    dispatch(z, 1)

    fakes = ((0, xf), (1, df))

    def fake_yh(i, ref):
        landed(ref.at[:, cols(z, 0)], fd_recv.at[i])
        remote(ref.at[:, cols(z, 0)], ref.at[:, cols(z, 0)], f_send.at[i], f_yh.at[i], other)

    def fake_own(i, ref, sub):
        if sub == 1:
            landed(ref.at[:, cols(z, 1)], f_yh.at[i])
        for way in (0, 1):
            ring_send(ref, z, sub, way, 1, f_send.at[i], f_recv.at[i])

    def fake_step(i, ref, dist, sub):
        ring_take(ref, dist, sub, f_send.at[i], f_recv.at[i])

    fake_yh(0, xf)
    fake_own(0, xf, 0)
    fake_yh(1, df)
    real_step(1, 0)
    real_step(1, 1)
    fake_own(0, xf, 1)
    real_step(2, 0)
    real_step(2, 1)
    fake_step(0, xf, 1, 0)
    real_step(3, 0)
    real_step(3, 1)
    real_step(4, 0)
    real_step(4, 1)
    local(sent.at[block(e), :], rows.at[block(e), :], rd_recv)
    fake_step(0, xf, 1, 1)
    fake_own(1, df, 0)
    fake_step(0, xf, 2, 0)
    fake_step(0, xf, 2, 1)
    fake_own(1, df, 1)
    fake_step(0, xf, 3, 0)
    fake_step(0, xf, 3, 1)

    chunk = 256
    for i, (src, dst) in enumerate(((wru_hbm, wru), (wrd_hbm, wrd), (wfu_hbm, wfu), (wfd_hbm, wfd))):
        pltpu.make_async_copy(src, dst, w_sem.at[i]).wait()
    landed(rows, rd_recv)

    def up(r, _):
        at = pl.ds(pl.multiple_of(r * chunk, chunk), chunk)
        pre = jnp.dot(rows[at, :], wru[...], preferred_element_type=F32)
        hidden[at, :] = gelu_tanh(pre).astype(BF)
        return 0

    lax.fori_loop(0, total // chunk, up, 0)

    def down(step):
        zz = near(1 + step)
        w = jnp.concatenate([wrd[:, cols(zz, 0)], wrd[:, cols(zz, 1)]], axis=1)

        def part(r, _):
            at = pl.ds(pl.multiple_of(r * chunk, chunk), chunk)
            got = jnp.dot(hidden[at, :], w, preferred_element_type=F32).astype(BF)
            po[at, cols(zz, 0)] = got[:, :128]
            po[at, cols(zz, 1)] = got[:, 128:]
            return 0

        lax.fori_loop(0, total // chunk, part, 0)

    def give_back(step):
        zz = near(1 + step)
        for sub in (0, 1):

            def give(k, _, sub=sub):
                to = (e + k) % ne
                remote(
                    po.at[block(to), cols(zz, sub)],
                    ret.at[block(e), cols(zz, sub)],
                    rt_send,
                    rt_recv.at[step, sub],
                    (to, t, dp),
                )
                return 0

            lax.fori_loop(1, ne, give, 0)
            local(po.at[block(e), cols(zz, sub)], ret.at[block(e), cols(zz, sub)], rt_recv.at[step, sub])

    down(0)
    for step in range(1, nz):
        down(step)
        give_back(step - 1)
    give_back(nz - 1)

    def combine(step):
        zz = near(1 + step)
        for sub in (0, 1):
            landed(ret.at[:, cols(zz, sub)], rt_recv.at[step, sub])
        got = jnp.concatenate([ret[:, cols(zz, 0)], ret[:, cols(zz, 1)]], axis=1)
        both = jnp.dot(high_ref[...], got, preferred_element_type=F32) + jnp.dot(
            low_ref[...], got, preferred_element_type=F32
        )
        both = both.astype(BF)
        cs[:, cols(zz, 0)] = both[:, :128]
        cs[:, cols(zz, 1)] = both[:, 128:]

    def reduce_send(step):
        zz = near(1 + step)
        for sub in (0, 1):
            if step == nz - 1 and sub == 0:
                local(cs.at[:, cols(zz, 0)], rs.at[t], rs_recv)
            else:
                y = yh if sub == 0 else oy
                remote(cs.at[:, cols(zz, sub)], rs.at[t], rs_send, rs_recv, (e, y * nz + zz, dp))

    mine = pl.ds(pl.multiple_of(dp * wide, 128), wide)
    theirs = pl.ds(pl.multiple_of((1 - dp) * wide, 128), wide)

    fake_step(0, xf, 4, 0)
    fake_step(0, xf, 4, 1)
    remote(xf.at[:, theirs], px, dp_send.at[0], dp_recv.at[0], mate)
    fake_step(1, df, 1, 0)

    def fake_up(r, _):
        at = pl.ds(pl.multiple_of(r * chunk, chunk), chunk)
        pre = jnp.dot(xf[at, :], wfu[...], preferred_element_type=F32)
        a, s = gelu_both(pre)
        act[at, :] = a.astype(BF)
        slope[at, :] = s
        return 0

    lax.fori_loop(0, total // chunk, fake_up, 0)
    fake_step(1, df, 1, 1)
    remote(act, pact, dp_send.at[1], dp_recv.at[1], mate)
    combine(0)
    fake_step(1, df, 2, 0)
    combine(1)
    reduce_send(0)
    fake_step(1, df, 2, 1)
    combine(2)
    reduce_send(1)
    fake_step(1, df, 3, 0)
    fake_step(1, df, 3, 1)
    combine(3)
    reduce_send(2)
    combine(4)
    reduce_send(3)
    combine(5)
    reduce_send(4)
    combine(6)
    reduce_send(5)
    combine(7)
    reduce_send(6)
    fake_step(1, df, 4, 0)
    fake_step(1, df, 4, 1)
    reduce_send(7)
    remote(df.at[:, theirs], pd, dp_send.at[2], dp_recv.at[2], mate)

    def fake_back(r, _):
        at = pl.ds(pl.multiple_of(r * chunk, chunk), chunk)
        back = lax.dot_general(
            df[at, :], wfd[...], (((1,), (1,)), ((), ())), preferred_element_type=F32
        )
        dpre[at, :] = (back * slope[at, :]).astype(BF)
        return 0

    lax.fori_loop(0, total // chunk, fake_back, 0)

    half = wide // 2

    for m in (0, 1):
        own = pl.ds(pl.multiple_of(dp * wide + m * half, 128), half)
        pl_m = pl.ds(m * half, half)
        if m == 0:
            landed(pact, dp_recv.at[1])
            landed(pd, dp_recv.at[2])
        gd_ref[:, pl_m] = (over_rows(act[...], df[:, own]) + over_rows(pact[...], pd[:, pl_m])).astype(BF)
        if m == 0:
            remote(dpre, pdpre, dp_send.at[3], dp_recv.at[3], mate)
    landed(px, dp_recv.at[0])
    landed(pdpre, dp_recv.at[3])
    for m in (0, 1):
        own = pl.ds(pl.multiple_of(dp * wide + m * half, 128), half)
        pl_m = pl.ds(m * half, half)
        gu_ref[pl_m, :] = (over_rows(xf[:, own], dpre[...]) + over_rows(px[:, pl_m], pdpre[...])).astype(BF)

    landed(rs, rs_recv)
    summed = rs[0].astype(F32)
    for i in range(1, 2 * nz):
        summed = summed + rs[i].astype(F32)
    out_ref[...] = summed.astype(BF)

    most = pl.ds(0, (2 * nz - 1) * 128)
    seven = pl.ds(0, (ne - 1) * cap)
    landed(xt.at[:, most], xt_send)
    for i, src in enumerate((sx_ref, sd_ref)):
        landed(src.at[seven, :], fd_send.at[i])
    for i, ref in fakes:
        landed(ref.at[:, most], f_send.at[i])
    landed(sent.at[seven, :], rd_send)
    landed(po.at[seven, :], rt_send)
    landed(cs.at[:, most], rs_send)
    landed(px, dp_send.at[0])
    landed(act, dp_send.at[1])
    landed(pd, dp_send.at[2])
    landed(dpre, dp_send.at[3])


def solution(mesh):
    ne, nt = mesh.shape["expert"], mesh.shape["tensor"]
    nz = nt // 2

    def on_device(
        x_real,
        routes_real,
        gates_real,
        up_real,
        down_real,
        x_fake,
        routes_fake,
        gates_fake,
        cotangent,
        up_fake,
        down_fake,
    ):
        tokens, part = x_real.shape
        cap = tokens // 2
        total = ne * cap
        width = up_real.shape[1]
        ff = up_real.shape[2]
        half = width // 2
        real_pos = slot_index(routes_real, ne, cap)
        slots = jnp.arange(total, dtype=jnp.int32)
        flipped = real_pos.T
        spread = (
            (flipped[0][None, :] == slots[:, None]) | (flipped[1][None, :] == slots[:, None])
        ).astype(BF)
        match = (real_pos[:, :, None] == slots[None, None, :]).astype(F32)
        weights = jnp.sum(match * gates_real[:, :, None], axis=1)
        high = weights.astype(BF)
        low = (weights - high.astype(F32)).astype(BF)
        fake_pos = slot_index(routes_fake, ne, cap)
        sx = over_rows(spread_matrix(fake_pos, total), x_fake).astype(BF)
        sd = over_rows(pick_matrix(fake_pos, total), scale_rows(gates_fake, cotangent)).astype(BF)
        vmem = pl.BlockSpec(memory_space=pltpu.VMEM)
        hbm = pl.BlockSpec(memory_space=pl.ANY)
        dma = pltpu.SemaphoreType.DMA
        real_out, grad_up, grad_down = pl.pallas_call(
            functools.partial(kernel, (ne, nz, cap)),
            out_shape=(
                jax.ShapeDtypeStruct((tokens, part), BF),
                jax.ShapeDtypeStruct((half, ff), BF),
                jax.ShapeDtypeStruct((ff, half), BF),
            ),
            in_specs=[vmem] * 6 + [hbm] * 4,
            out_specs=(vmem, vmem, vmem),
            scratch_shapes=[
                pltpu.VMEM((width, ff), BF),
                pltpu.VMEM((ff, width), BF),
                pltpu.VMEM((width, ff), BF),
                pltpu.VMEM((ff, width), BF),
                pltpu.VMEM((tokens, width), BF),
                pltpu.VMEM((total, width), BF),
                pltpu.VMEM((total, width), BF),
                pltpu.VMEM((total, width), BF),
                pltpu.VMEM((total, width), BF),
                pltpu.VMEM((total, width), BF),
                pltpu.VMEM((total, width), BF),
                pltpu.VMEM((total, half), BF),
                pltpu.VMEM((total, half), BF),
                pltpu.VMEM((total, ff), BF),
                pltpu.VMEM((total, ff), BF),
                pltpu.VMEM((total, ff), BF),
                pltpu.VMEM((total, ff), BF),
                pltpu.VMEM((total, ff), F32),
                pltpu.VMEM((total, ff), BF),
                pltpu.VMEM((tokens, width), BF),
                pltpu.VMEM((nt, tokens, part), BF),
                dma((4,)),
                dma,
                dma,
                dma,
                dma((2, nz // 2, 2)),
                dma((2,)),
                dma((2,)),
                dma((2,)),
                dma((2,)),
                dma((2, 2, nz // 2, 2)),
                dma,
                dma,
                dma,
                dma((nz, 2)),
                dma,
                dma,
                dma((4,)),
                dma((4,)),
            ],
            compiler_params=pltpu.CompilerParams(
                collective_id=0, has_side_effects=True, vmem_limit_bytes=62 * 1024 * 1024
            ),
        )(
            x_real,
            spread,
            high,
            low,
            sx,
            sd,
            up_real[0],
            down_real[0],
            up_fake[0],
            down_fake[0],
        )
        return real_out, grad_up[None], grad_down[None]

    placed = (
        P(("expert", "dp"), "tensor"),
        P(("expert", "dp"), None),
        P(("expert", "dp"), None),
        P("expert", None, "tensor"),
        P("expert", "tensor", None),
        P(("expert", "dp"), "tensor"),
        P(("expert", "dp"), None),
        P(("expert", "dp"), None),
        P(("expert", "dp"), "tensor"),
        P("expert", None, "tensor"),
        P("expert", "tensor", None),
    )
    return jax.shard_map(
        on_device,
        mesh=mesh,
        in_specs=placed,
        out_specs=(
            P(("expert", "dp"), "tensor"),
            P("expert", "dp", "tensor"),
            P("expert", "tensor", "dp"),
        ),
        check_vma=False,
    )
```

time: 415 us -> 175 us (0.42)
  waiting for transfers between devices: 274 us -> 0 us
  Pallas kernels: 0 us -> 156 us
  matrix products: 50.7 us -> 2.67 us
  starting transfers between devices: 27.9 us -> 0 us
  local copies, waits for them, and re-layouts: 29.3 us -> 7.4 us
  between operations: 15.7 us -> 0.72 us
  other arithmetic: 15 us -> 8.21 us
    all_to_all x4 -> x0, waiting for transfers between devices: 192 us -> none  [the longest x1 115 us: in_one_piece(): lax.all_to_all(both, axis, split_axis=split_dim, concat_axis=concat_dim,...]
    pallas_call x0 -> x1, Pallas kernels: none -> 156 us  [on_device(): pl.pallas_call(functools.partial(kernel, (ne, nz, cap)), out_shape=(jax.S...]
    all_gather x1 -> x0, waiting for transfers between devices: 79 us -> none  [sent_together(): lax.all_gather(both, axis, axis=dim, tiled=True)]
    dot_general x8 -> x0, matrix products: 34.8 us -> none  [the longest x3 13.5 us: to_slots(): lax.dot_general(matrix, rows, (((0,), (0,)), ((), ())), preferred_element...]
    all_to_all x4 -> x0, starting transfers between devices: 26.8 us -> none  [the longest x1 11.2 us: sent_to_all(): return lax.all_to_all(copies, axis, split_axis=0, concat_axis=0, tiled=True)]
    dot_general x4 -> x2, matrix products: 15.9 us -> 2.67 us  [over_rows(): lax.dot_general(left, right, (((0,), (0,)), ((), ())), preferred_element_...]
    mul x3 -> x2, local copies, waits for them, and re-layouts: 10.6 us -> 1.06 us  [scale_rows(): scaled = gates[:, :, None] * rows[:, None, :].astype(F32)]
    concatenate x2 -> x0, other arithmetic: 9 us -> none  [the longest x1 8.34 us: in_one_piece(): both = jnp.concatenate(arrays, axis=along)]
  transfers between devices with their start and end apart: 11 -> 0, of which waited for: 6 -> 0; matrix products, arithmetic and copies ran while one was open for 21% -> 0% of each run, Pallas kernels for 0% -> 0%
where the time goes in v2:
time: 175 us
  Pallas kernels  156 us (89%)
  other arithmetic  8.21 us (5%)
  local copies, waits for them, and re-layouts  7.4 us (4%)
  matrix products  2.67 us (2%)
    pallas_call x1, Pallas kernels, on_device(): pl.pallas_call(functools.partial(kernel, (ne, nz, cap)), out_shape=(jax.S...  156 us
    unnamed x10, local copies, waits for them, and re-layouts  5.62 us

profile of v2, /device:TPU:6, one launch (start us, length us, event | category | flops | bytes accessed | tf_op | source)
XLA Modules:
  0.0 174.9 jit_solution(69612604380269100)
XLA Ops:
  0.6 0.0 copy-start
  0.6 0.0 copy-start.2
  0.7 0.7 convert_reduce_fusion.2
  1.4 0.6 reduce-window.14
  1.9 0.2 slice_reduce_fusion.1
  2.2 0.1 bitcast_subtract_fusion.1
  2.3 0.7 select_reduce_fusion.2
  3.0 0.7 multiply_add_fusion.1
  3.7 0.7 convert_reduce_fusion.1
  4.4 0.6 reduce-window.16
  4.9 0.2 slice_reduce_fusion
  5.2 0.1 bitcast_subtract_fusion
  5.3 0.7 select_reduce_fusion.1
  6.0 0.7 multiply_add_fusion
  6.7 0.1 copy.28
  6.8 0.1 eq.117
  7.0 0.8 copy.29
  7.8 0.1 mul.56
  7.9 0.9 mul.58
  8.8 1.6 fusion.1.sd_ref
  10.4 0.3 convert_reduce_fusion
  10.7 0.0 copy-done
  10.7 1.1 convolution_convert_fusion.sx_ref
  11.8 1.0 fusion.4.spread_ref
  12.8 0.0 copy-done.2
  12.8 0.3 select_reduce_fusion
  13.1 1.1 subtract_convert_fusion
  14.2 155.9 %shard_map.130 = (bf16[256,128]{1,0:T(8,128)(2,1)}, bf16[1024,512]{1,0:T(8,128)(2,1)}, bf16[512,1024]{1,0:T(8,128)(2,1)}) custom-call(bf16[256,128]{1,0:T(8,128)(2,1)} %xr_ref.1, bf16[1024,256]{1,0:T(8,128)(2,1)} %fusion.4.spread_ref, bf16[256,1024]{1,0:T(8,128)(2,1)} %get-tuple-element.10.high_ref, bf16[256,1024]{1,0:T(8,128)(2,1)} %get-tuple-element.9.low_ref, ...), custom_call_target="tpu_custom_call" | custom-call | tf_op jit(solution)/shard_map/pallas_call | solution.py:496
  170.1 0.0 copy-start.1
  170.1 1.6 copy.33
  171.7 2.3 %copy.34 = bf16[1,1024,512]{2,1,0:T(8,128)(2,1)} copy(bf16[1,1024,512]{2,1,0:T(8,128)(2,1)} %bitcast.31) | data formatting | bytes 2097152
  173.9 0.0 copy-done.1
  173.9 1.0 copy.35
  (5 shorter events, 0.1 us)
Async XLA Ops:
  0.6 10.1 %copy-start = (bf16[256,128]{1,0:T(8,128)(2,1)S(1)}, bf16[256,128]{1,0:T(8,128)(2,1)}, u32[]{:S(2)}) copy-start(bf16[256,128]{1,0:T(8,128)(2,1)} %param.16) | copy-start | bytes 196612
  0.6 12.1 %copy-start.2 = (f32[256,2]{0,1:T(2,128)S(1)}, f32[256,2]{0,1:T(2,128)}, u32[]{:S(2)}) copy-start(f32[256,2]{0,1:T(2,128)} %param.13) | copy-start | bytes 6148
  170.1 3.8 %copy-start.1 = (bf16[512,1024]{1,0:T(8,128)(2,1)S(1)}, bf16[512,1024]{1,0:T(8,128)(2,1)}, u32[]{:S(2)}) copy-start(bf16[512,1024]{1,0:T(8,128)(2,1)} %get-tuple-element.8) | copy-start | bytes 3145732

commit v3 on v2

v3 whole, which is shorter than its diff:
```python
import functools

import jax
import jax.numpy as jnp
from jax import lax
from jax.experimental import pallas as pl
from jax.experimental.pallas import tpu as pltpu
from jax.sharding import PartitionSpec as P

MESH = pl.DeviceIdType.MESH
BF = jnp.bfloat16
F32 = jnp.float32

slope_const = 0.7978845608028654
cubic_coef = 0.044715


def gelu_tanh(value):
    return (
        0.5 * value * (1.0 + jnp.tanh(slope_const * (value + cubic_coef * value * value * value)))
    )


def gelu_both(value):
    square = value * value
    inner = jnp.tanh(slope_const * (value + cubic_coef * square * value))
    act = 0.5 * value * (1.0 + inner)
    slope = 0.5 * (1.0 + inner) + 0.5 * value * (1.0 - inner * inner) * slope_const * (
        1.0 + 3.0 * cubic_coef * square
    )
    return act, slope


def over_rows(left, right):
    return lax.dot_general(left, right, (((0,), (0,)), ((), ())), preferred_element_type=F32)


def kernel(
    sizes,
    xr_ref,
    xk_ref,
    ct_ref,
    rr_ref,
    gr_ref,
    rf_ref,
    gf_ref,
    wru_hbm,
    wrd_hbm,
    wfu_hbm,
    wfd_hbm,
    out_ref,
    gu_ref,
    gd_ref,
    wru,
    wrd,
    wfu,
    wfd,
    spread,
    wt,
    high,
    low,
    sx,
    sd,
    xt,
    sent,
    rows,
    po,
    ret,
    xf,
    df,
    px,
    pd,
    act_t,
    pact_t,
    dpre,
    pdpre,
    slope,
    acc,
    hidden,
    cs,
    rs,
    mine_f,
    last,
    w_sem,
    loc_sem,
    xt_send,
    xt_yh,
    xt_recv,
    fd_send,
    fd_recv,
    f_send,
    f_recv,
    rd_send,
    rd_recv,
    rt_send,
    rt_recv,
    rs_send,
    rs_recv,
    la_send,
    la_recv,
    px_send,
    px_recv,
    pd_send,
    pd_recv,
    dp_send,
    dp_recv,
):
    ne, nz, cap = sizes
    e = lax.axis_index("expert")
    t = lax.axis_index("tensor")
    dp = lax.axis_index("dp")
    yh = t // nz
    z = t % nz
    oy = 1 - yh
    wide = nz * 128
    total = ne * cap

    def near(step):
        return (z + step + nz) % nz

    def cols(zz, sub):
        y = yh if sub == 0 else oy
        return pl.ds(pl.multiple_of(y * wide + zz * 128, 128), 128)

    def block(expert):
        return pl.ds(pl.multiple_of(expert * cap, cap), cap)

    def remote(src, dst, send, recv, where):
        pltpu.make_async_remote_copy(
            src_ref=src, dst_ref=dst, send_sem=send, recv_sem=recv, device_id=where, device_id_type=MESH
        ).start()

    def local(src, dst, sem):
        pltpu.make_async_copy(src, dst, sem).start()

    def landed(ref, sem):
        pltpu.make_async_copy(ref, ref, sem).wait()

    other = (e, oy * nz + z, dp)
    mate = (e, t, 1 - dp)
    sides = ((e, yh * nz + near(1), dp), (e, yh * nz + near(-1), dp))

    barrier = pltpu.get_barrier_semaphore()

    def greet_expert(k, _):
        for y in (yh, oy):
            pl.semaphore_signal(
                barrier, inc=1, device_id=((e + k) % ne, y * nz + z, dp), device_id_type=MESH
            )
        return 0

    def greet_tensor(k, _):
        pl.semaphore_signal(
            barrier, inc=1, device_id=(e, (t + k) % (2 * nz), dp), device_id_type=MESH
        )
        return 0

    lax.fori_loop(1, ne, greet_expert, 0)
    lax.fori_loop(1, 2 * nz, greet_tensor, 0)
    pl.semaphore_signal(barrier, inc=1, device_id=mate, device_id_type=MESH)
    local(xr_ref, xt.at[:, cols(z, 0)], loc_sem)
    for i, (src, dst) in enumerate(((wru_hbm, wru), (wrd_hbm, wrd), (wfu_hbm, wfu), (wfd_hbm, wfd))):
        local(src, dst, w_sem.at[i])

    tokens = xr_ref.shape[0]
    chunk = 256
    earlier = (
        lax.broadcasted_iota(jnp.int32, (tokens, tokens), 0)
        < lax.broadcasted_iota(jnp.int32, (tokens, tokens), 1)
    ).astype(F32).astype(BF)
    labels = lax.broadcasted_iota(jnp.int32, (2 * ne, tokens), 0)

    def places(routes):
        hits = [(labels == routes[k : k + 1, :]).astype(F32) for k in (0, 1)]
        before = jnp.dot(
            (hits[0] + hits[1]).astype(BF), earlier, preferred_element_type=F32
        )
        return [
            routes[k : k + 1, :] * cap
            + jnp.sum(hits[k] * before, axis=0, keepdims=True).astype(jnp.int32)
            for k in (0, 1)
        ]

    def matches(at, places_of):
        slots = at * chunk + lax.broadcasted_iota(jnp.int32, (chunk, tokens), 0)
        return [slots == p for p in places_of]

    def weigh(masks, gates):
        return jnp.where(masks[0], gates[0:1, :], 0.0) + jnp.where(masks[1], gates[1:2, :], 0.0)

    fake_places = places(rf_ref[...])

    def fake_slots(r, _):
        at = pl.ds(pl.multiple_of(r * chunk, chunk), chunk)
        masks = matches(r, fake_places)
        pick = (masks[0] | masks[1]).astype(F32).astype(BF)
        sx[at, :] = jnp.dot(pick, xk_ref[...], preferred_element_type=F32).astype(BF)
        gate = jnp.sum(weigh(masks, gf_ref[...]), axis=1, keepdims=True)
        sd[at, :] = (gate * jnp.dot(pick, ct_ref[...], preferred_element_type=F32)).astype(BF)
        return 0

    lax.fori_loop(0, total // chunk, fake_slots, 0)
    real_places = places(rr_ref[...])

    def real_slots(r, _):
        at = pl.ds(pl.multiple_of(r * chunk, chunk), chunk)
        masks = matches(r, real_places)
        spread[at, :] = (masks[0] | masks[1]).astype(F32).astype(BF)
        wt[at, :] = weigh(masks, gr_ref[...])
        return 0

    lax.fori_loop(0, total // chunk, real_slots, 0)
    pl.semaphore_wait(barrier, 2 * (ne - 1) + 2 * nz)

    def ring_send(ref, zz, sub, way, dist, send, recv):
        remote(
            ref.at[:, cols(zz, sub)],
            ref.at[:, cols(zz, sub)],
            send,
            recv.at[way, dist - 1, sub],
            sides[way],
        )

    def ring_take(ref, dist, sub, send, recv):
        for way in (0, 1):
            if dist == nz // 2 and way != sub:
                continue
            zz = near(-dist if way == 0 else dist)
            landed(ref.at[:, cols(zz, sub)], recv.at[way, dist - 1, sub])
            if dist < nz // 2 - 1 or (dist == nz // 2 - 1 and way == sub):
                ring_send(ref, zz, sub, way, dist + 1, send, recv)

    local_x = pltpu.make_async_copy(xr_ref, xt.at[:, cols(z, 0)], loc_sem)
    local_x.wait()
    for way in (0, 1):
        ring_send(xt, z, 0, way, 1, xt_send, xt_recv)
    remote(xt.at[:, cols(z, 0)], xt.at[:, cols(z, 0)], xt_send, xt_yh, other)

    def fake_give(i, src, dst):
        for far, y in ((0, yh), (1, oy)):

            def give(k, _, far=far, y=y):
                to = (e + k) % ne
                remote(
                    src.at[block(to), :],
                    dst.at[block(e), cols(z, 0)],
                    fd_send.at[i, far],
                    fd_recv.at[i, far],
                    (to, y * nz + z, dp),
                )
                return 0

            lax.fori_loop(1 - far, ne, give, 0)
        local(src.at[block(e), :], dst.at[block(e), cols(z, 0)], fd_recv.at[i, 0])

    fake_give(0, sx, xf)

    def slot(zz, sub):
        sent[:, cols(zz, sub)] = jnp.dot(
            spread[...], xt[:, cols(zz, sub)], preferred_element_type=F32
        ).astype(BF)

    def dispatch(zz, sub):
        def give(k, _):
            to = (e + k) % ne
            remote(
                sent.at[block(to), cols(zz, sub)],
                rows.at[block(e), cols(zz, sub)],
                rd_send,
                rd_recv,
                (to, t, dp),
            )
            return 0

        lax.fori_loop(1, ne, give, 0)

    def real_step(dist, sub):
        ring_take(xt, dist, sub, xt_send, xt_recv)
        if dist == nz // 2:
            slot(near(dist), sub)
            dispatch(near(dist), sub)
        else:
            slot(near(-dist), sub)
            slot(near(dist), sub)
            dispatch(near(-dist), sub)
            dispatch(near(dist), sub)

    slot(z, 0)
    landed(xt.at[:, cols(z, 1)], xt_yh)
    for way in (0, 1):
        ring_send(xt, z, 1, way, 1, xt_send, xt_recv)
    slot(z, 1)
    dispatch(z, 0)
    dispatch(z, 1)

    fakes = ((0, xf), (1, df))

    def fake_own(i, ref, sub):
        landed(ref.at[:, cols(z, sub)], fd_recv.at[i, sub])
        for way in (0, 1):
            ring_send(ref, z, sub, way, 1, f_send.at[i], f_recv.at[i])

    def fake_step(i, ref, dist, sub):
        ring_take(ref, dist, sub, f_send.at[i], f_recv.at[i])

    for dist in (1, 2, 3):
        real_step(dist, 0)
        real_step(dist, 1)
    fake_own(0, xf, 0)
    fake_own(0, xf, 1)
    real_step(4, 0)
    real_step(4, 1)
    local(sent.at[block(e), :], rows.at[block(e), :], rd_recv)
    fake_give(1, sd, df)
    weights = wt[...].T
    rounded = weights.astype(BF)
    high[...] = rounded
    low[...] = (weights - rounded.astype(F32)).astype(BF)
    fake_step(0, xf, 1, 0)
    fake_step(0, xf, 1, 1)
    fake_step(0, xf, 2, 0)
    fake_step(0, xf, 2, 1)
    fake_step(0, xf, 3, 0)
    fake_step(0, xf, 3, 1)

    for i, (src, dst) in enumerate(((wru_hbm, wru), (wrd_hbm, wrd), (wfu_hbm, wfu), (wfd_hbm, wfd))):
        pltpu.make_async_copy(src, dst, w_sem.at[i]).wait()
    landed(rows, rd_recv)

    def up(r, _):
        at = pl.ds(pl.multiple_of(r * chunk, chunk), chunk)
        pre = jnp.dot(rows[at, :], wru[...], preferred_element_type=F32)
        hidden[at, :] = gelu_tanh(pre).astype(BF)
        return 0

    lax.fori_loop(0, total // chunk, up, 0)

    turns = [nz // 2] + [way * d for d in range(nz // 2 - 1, 0, -1) for way in (-1, 1)] + [0]

    def down(step):
        zz = near(turns[step])
        w = jnp.concatenate([wrd[:, cols(zz, 0)], wrd[:, cols(zz, 1)]], axis=1)

        def part(r, _):
            at = pl.ds(pl.multiple_of(r * chunk, chunk), chunk)
            got = jnp.dot(hidden[at, :], w, preferred_element_type=F32).astype(BF)
            po[at, cols(zz, 0)] = got[:, :128]
            po[at, cols(zz, 1)] = got[:, 128:]
            return 0

        lax.fori_loop(0, total // chunk, part, 0)

    def give_back(step):
        zz = near(turns[step])
        for sub in (0, 1):

            def give(k, _, sub=sub):
                to = (e + k) % ne
                remote(
                    po.at[block(to), cols(zz, sub)],
                    ret.at[block(e), cols(zz, sub)],
                    rt_send,
                    rt_recv.at[step, sub],
                    (to, t, dp),
                )
                return 0

            lax.fori_loop(1, ne, give, 0)
            local(po.at[block(e), cols(zz, sub)], ret.at[block(e), cols(zz, sub)], rt_recv.at[step, sub])

    down(0)
    for step in range(1, nz):
        down(step)
        give_back(step - 1)
        if step == 2:
            fake_own(1, df, 0)
        if step == 5:
            fake_own(1, df, 1)
    give_back(nz - 1)

    def combine(step):
        turn = turns[step]
        dist = abs(turn)
        zz = near(turn)
        for sub in (0, 1):
            landed(ret.at[:, cols(zz, sub)], rt_recv.at[step, sub])
        got = jnp.concatenate([ret[:, cols(zz, 0)], ret[:, cols(zz, 1)]], axis=1)
        both = jnp.dot(high[...], got, preferred_element_type=F32) + jnp.dot(
            low[...], got, preferred_element_type=F32
        )
        left, right = pl.ds(0, 128), pl.ds(128, 128)
        if dist == nz // 2:
            cs[step] = both.astype(BF)
            for way, half in ((0, left), (1, right)):
                remote(
                    cs.at[step, :, half],
                    rs.at[way, dist - 1, :, half],
                    rs_send,
                    rs_recv.at[way, dist - 1],
                    sides[way],
                )
        elif dist > 0:
            way = 0 if turn > 0 else 1
            if dist == nz // 2 - 1:
                half = (left, right)[way]
                landed(rs.at[way, dist, :, half], rs_recv.at[way, dist])
                cs[step] = both.astype(BF)
                more = both[:, way * 128 : (way + 1) * 128] + rs[way, dist, :, half].astype(F32)
                cs[step, :, half] = more.astype(BF)
            else:
                landed(rs.at[way, dist], rs_recv.at[way, dist])
                cs[step] = (both + rs[way, dist].astype(F32)).astype(BF)
            remote(
                cs.at[step], rs.at[way, dist - 1], rs_send, rs_recv.at[way, dist - 1], sides[way]
            )
        else:
            for way in (0, 1):
                landed(rs.at[way, 0], rs_recv.at[way, 0])
            both = both + rs[0, 0].astype(F32) + rs[1, 0].astype(F32)
            mine_f[...] = both[:, :128]
            cs[step, :, right] = both[:, 128:].astype(BF)
            remote(cs.at[step, :, right], last, la_send, la_recv, other)

    def half_cols(zz, side):
        return pl.ds(pl.multiple_of(side * wide + zz * 128, 128), 128)

    def fake_up(r, _):
        at = pl.ds(pl.multiple_of(r * chunk, chunk), chunk)
        pre = jnp.dot(xf[at, :], wfu[...], preferred_element_type=F32)
        a, s = gelu_both(pre)
        act_t[:, at] = a.T.astype(BF)
        slope[at, :] = s
        return 0

    def fake_mate(dist):
        for n, zz in enumerate(pair_of(dist)):
            at = pl.ds(pl.multiple_of(zz * 128, 128), 128)
            remote(df.at[:, half_cols(zz, 1 - dp)], pd.at[:, at], pd_send, pd_recv.at[dist, n], mate)

    def pair_of(dist):
        return (near(dist),) if dist in (0, nz // 2) else (near(-dist), near(dist))

    def back_part(dist):
        for zz in pair_of(dist):
            w = jnp.concatenate([wfd[:, cols(zz, 0)], wfd[:, cols(zz, 1)]], axis=1)

            def part(r, _, zz=zz, w=w):
                at = pl.ds(pl.multiple_of(r * chunk, chunk), chunk)
                rows_d = jnp.concatenate([df[at, cols(zz, 0)], df[at, cols(zz, 1)]], axis=1)
                back = lax.dot_general(
                    rows_d, w, (((1,), (1,)), ((), ())), preferred_element_type=F32
                )
                if dist == 0:
                    acc[at, :] = back
                elif dist == nz // 2:
                    dpre[at, :] = ((acc[at, :] + back) * slope[at, :]).astype(BF)
                else:
                    acc[at, :] += back
                return 0

            lax.fori_loop(0, total // chunk, part, 0)

    def grad_down_part(dist):
        zs = pair_of(dist)
        ats = [pl.ds(pl.multiple_of(zz * 128, 128), 128) for zz in zs]
        for n, at in enumerate(ats):
            landed(pd.at[:, at], pd_recv.at[dist, n])
        own = [df[:, half_cols(zz, dp)] for zz in zs]
        got = [pd[:, at] for at in ats]
        if len(zs) == 2:
            own, got = [jnp.concatenate(own, axis=1)], [jnp.concatenate(got, axis=1)]
        grad = jnp.dot(act_t[...], own[0], preferred_element_type=F32) + jnp.dot(
            pact_t[...], got[0], preferred_element_type=F32
        )
        grad = grad.astype(BF)
        for n, at in enumerate(ats):
            gd_ref[:, at] = grad[:, n * 128 : (n + 1) * 128]

    theirs = pl.ds(pl.multiple_of((1 - dp) * wide, 128), wide)

    fake_step(0, xf, 4, 0)
    fake_step(0, xf, 4, 1)
    remote(xf.at[:, theirs], px, px_send, px_recv, mate)
    lax.fori_loop(0, total // chunk, fake_up, 0)
    fake_step(1, df, 1, 0)
    combine(0)
    remote(act_t, pact_t, dp_send.at[0], dp_recv.at[0], mate)
    fake_mate(0)
    fake_step(1, df, 1, 1)
    fake_mate(1)
    combine(1)
    back_part(0)
    back_part(1)
    combine(2)
    fake_step(1, df, 2, 0)
    landed(pact_t, dp_recv.at[0])
    grad_down_part(0)
    grad_down_part(1)
    combine(3)
    fake_step(1, df, 2, 1)
    fake_mate(2)
    combine(4)
    back_part(2)
    fake_step(1, df, 3, 0)
    combine(5)
    grad_down_part(2)
    fake_step(1, df, 3, 1)
    fake_mate(3)
    combine(6)
    back_part(3)
    grad_down_part(3)
    combine(7)
    fake_step(1, df, 4, 0)
    fake_step(1, df, 4, 1)
    fake_mate(4)
    back_part(4)
    remote(dpre, pdpre, dp_send.at[1], dp_recv.at[1], mate)
    grad_down_part(4)
    landed(px, px_recv)
    half = wide // 2
    for m in (0, 1):
        own = pl.ds(pl.multiple_of(dp * wide + m * half, 128), half)
        acc[m * half : (m + 1) * half, :] = over_rows(xf[:, own], dpre[...])
    landed(last, la_recv)
    out_ref[...] = (mine_f[...] + last[...].astype(F32)).astype(BF)
    landed(pdpre, dp_recv.at[1])
    for m in (0, 1):
        at = slice(m * half, (m + 1) * half)
        gu_ref[at, :] = (acc[at, :] + over_rows(px[:, at], pdpre[...])).astype(BF)

    most = pl.ds(0, (2 * nz - 1) * 128)
    seven = pl.ds(0, (ne - 1) * cap)
    landed(xt.at[:, most], xt_send)
    for i, src in enumerate((sx, sd)):
        landed(src.at[seven, :], fd_send.at[i, 0])
        landed(src, fd_send.at[i, 1])
    for i, ref in fakes:
        landed(ref.at[:, pl.ds(0, (2 * nz - 2) * 128)], f_send.at[i])
    landed(sent.at[seven, :], rd_send)
    landed(po.at[seven, :], rt_send)
    landed(cs.at[pl.ds(0, nz - 1)], rs_send)
    landed(last, la_send)
    landed(px, px_send)
    landed(pd, pd_send)
    landed(act_t, dp_send.at[0])
    landed(dpre, dp_send.at[1])


def solution(mesh):
    ne, nt = mesh.shape["expert"], mesh.shape["tensor"]
    nz = nt // 2

    def on_device(
        x_real,
        routes_real,
        gates_real,
        up_real,
        down_real,
        x_fake,
        routes_fake,
        gates_fake,
        cotangent,
        up_fake,
        down_fake,
    ):
        tokens, part = x_real.shape
        cap = tokens // 2
        total = ne * cap
        width = up_real.shape[1]
        ff = up_real.shape[2]
        half = width // 2
        vmem = pl.BlockSpec(memory_space=pltpu.VMEM)
        hbm = pl.BlockSpec(memory_space=pl.ANY)
        dma = pltpu.SemaphoreType.DMA
        real_out, grad_up, grad_down = pl.pallas_call(
            functools.partial(kernel, (ne, nz, cap)),
            out_shape=(
                jax.ShapeDtypeStruct((tokens, part), BF),
                jax.ShapeDtypeStruct((half, ff), BF),
                jax.ShapeDtypeStruct((ff, half), BF),
            ),
            in_specs=[vmem] * 7 + [hbm] * 4,
            out_specs=(vmem, vmem, vmem),
            scratch_shapes=[
                pltpu.VMEM((width, ff), BF),
                pltpu.VMEM((ff, width), BF),
                pltpu.VMEM((width, ff), BF),
                pltpu.VMEM((ff, width), BF),
                pltpu.VMEM((total, tokens), BF),
                pltpu.VMEM((total, tokens), F32),
                pltpu.VMEM((tokens, total), BF),
                pltpu.VMEM((tokens, total), BF),
                pltpu.VMEM((total, part), BF),
                pltpu.VMEM((total, part), BF),
                pltpu.VMEM((tokens, width), BF),
                pltpu.VMEM((total, width), BF),
                pltpu.VMEM((total, width), BF),
                pltpu.VMEM((total, width), BF),
                pltpu.VMEM((total, width), BF),
                pltpu.VMEM((total, width), BF),
                pltpu.VMEM((total, width), BF),
                pltpu.VMEM((total, half), BF),
                pltpu.VMEM((total, half), BF),
                pltpu.VMEM((ff, total), BF),
                pltpu.VMEM((ff, total), BF),
                pltpu.VMEM((total, ff), BF),
                pltpu.VMEM((total, ff), BF),
                pltpu.VMEM((total, ff), F32),
                pltpu.VMEM((total, ff), F32),
                pltpu.VMEM((total, ff), BF),
                pltpu.VMEM((nz, tokens, 2 * part), BF),
                pltpu.VMEM((2, nz // 2, tokens, 2 * part), BF),
                pltpu.VMEM((tokens, part), F32),
                pltpu.VMEM((tokens, part), BF),
                dma((4,)),
                dma,
                dma,
                dma,
                dma((2, nz // 2, 2)),
                dma((2, 2)),
                dma((2, 2)),
                dma((2,)),
                dma((2, 2, nz // 2, 2)),
                dma,
                dma,
                dma,
                dma((nz, 2)),
                dma,
                dma((2, nz // 2)),
                dma,
                dma,
                dma,
                dma,
                dma,
                dma((nz // 2 + 1, 2)),
                dma((2,)),
                dma((2,)),
            ],
            compiler_params=pltpu.CompilerParams(
                collective_id=0, has_side_effects=True, vmem_limit_bytes=62 * 1024 * 1024
            ),
        )(
            x_real,
            x_fake,
            cotangent,
            routes_real.T,
            gates_real.T,
            routes_fake.T,
            gates_fake.T,
            up_real[0],
            down_real[0],
            up_fake[0],
            down_fake[0],
        )
        return real_out, grad_up[None], grad_down[None]

    placed = (
        P(("expert", "dp"), "tensor"),
        P(("expert", "dp"), None),
        P(("expert", "dp"), None),
        P("expert", None, "tensor"),
        P("expert", "tensor", None),
        P(("expert", "dp"), "tensor"),
        P(("expert", "dp"), None),
        P(("expert", "dp"), None),
        P(("expert", "dp"), "tensor"),
        P("expert", None, "tensor"),
        P("expert", "tensor", None),
    )
    return jax.shard_map(
        on_device,
        mesh=mesh,
        in_specs=placed,
        out_specs=(
            P(("expert", "dp"), "tensor"),
            P("expert", "dp", "tensor"),
            P("expert", "tensor", "dp"),
        ),
        check_vma=False,
    )
```

time: 175 us -> 139 us (0.79)
  Pallas kernels: 156 us -> 133 us
  other arithmetic: 8.21 us -> 0 us
  matrix products: 2.67 us -> 0 us
  local copies, waits for them, and re-layouts: 7.4 us -> 4.8 us
    pallas_call x1, Pallas kernels: 156 us -> 133 us  [on_device(): pl.pallas_call(functools.partial(kernel, (ne, nz, cap)), out_shape=(jax.S...]
    reduce_sum x6 -> x0, other arithmetic: 3.34 us -> none  [the longest x2 1.42 us: slot_index(): slots = jnp.sum(hits * before[:, None, :], axis=2)]
    dot_general x2 -> x0, matrix products: 2.67 us -> none  [over_rows(): lax.dot_general(left, right, (((0,), (0,)), ((), ())), preferred_element_...]
    convert_element_type x2 -> x0, other arithmetic: 2.14 us -> none  [the longest x1 1.12 us: on_device(): low = (weights - high.astype(F32)).astype(BF)]
    unnamed x10 -> x5, local copies, waits for them, and re-layouts: 5.62 us -> 4.8 us
where the time goes in v3:
time: 139 us; the launch traced here: 138 us
  Pallas kernels  133 us (96%)
  local copies, waits for them, and re-layouts  4.8 us (3%)
    pallas_call x1, Pallas kernels, on_device(): pl.pallas_call(functools.partial(kernel, (ne, nz, cap)), out_shape=(jax.S...  133 us
    unnamed x5, local copies, waits for them, and re-layouts  4.8 us

profile of v3, /device:TPU:6, one launch (start us, length us, event | category | flops | bytes accessed | tf_op | source)
XLA Modules:
  0.0 138.2 jit_solution(17471664507220537654)
XLA Ops:
  0.6 132.7 %shard_map.130 = (bf16[256,128]{1,0:T(8,128)(2,1)}, bf16[1024,512]{1,0:T(8,128)(2,1)}, bf16[512,1024]{1,0:T(8,128)(2,1)}) custom-call(bf16[256,128]{1,0:T(8,128)(2,1)} %xr_ref.1, bf16[256,128]{1,0:T(8,128)(2,1)} %xk_ref.1, bf16[256,128]{1,0:T(8,128)(2,1)} %ct_ref.1, s32[2,256]{1,0:T(2,128)} %bitcast.16, f32[2,256]{1,0:T(2,128)} %bitcast.17, ...), custom_call_target="tpu_custom_call" | custom-call | tf_op jit(solution)/shard_map/pallas_call | solution.py:575
  133.3 0.0 copy-start
  133.4 1.6 %copy.17 = bf16[256,128]{1,0:T(8,128)(2,1)} copy(bf16[256,128]{1,0:T(8,128)(2,1)} %get-tuple-element.12) | data formatting | bytes 131072
  134.9 2.3 %copy.18 = bf16[1,1024,512]{2,1,0:T(8,128)(2,1)} copy(bf16[1,1024,512]{2,1,0:T(8,128)(2,1)} %bitcast.15) | data formatting | bytes 2097152
  137.2 0.0 copy-done
  137.2 1.0 copy.19
Async XLA Ops:
  133.3 3.8 %copy-start = (bf16[512,1024]{1,0:T(8,128)(2,1)S(1)}, bf16[512,1024]{1,0:T(8,128)(2,1)}, u32[]{:S(2)}) copy-start(bf16[512,1024]{1,0:T(8,128)(2,1)} %get-tuple-element.8) | copy-start | bytes 3145732

commit v4 on v3

--- a/solution.py
+++ b/solution.py
@@ -48,9 +48,14 @@
     wrd_hbm,
     wfu_hbm,
     wfd_hbm,
+    out_hbm,
+    gu_hbm,
+    gd_hbm,
     out_ref,
     gu_ref,
     gd_ref,
+    xo_t,
+    px_t,
     wru,
     wrd,
     wfu,
@@ -82,6 +87,7 @@
     mine_f,
     last,
     w_sem,
+    o_sem,
     loc_sem,
     xt_send,
     xt_yh,
@@ -92,8 +98,10 @@
     f_recv,
     rd_send,
     rd_recv,
+    rh_recv,
     rt_send,
     rt_recv,
+    rth_recv,
     rs_send,
     rs_recv,
     la_send,
@@ -149,14 +157,9 @@
             )
         return 0
 
-    def greet_tensor(k, _):
-        pl.semaphore_signal(
-            barrier, inc=1, device_id=(e, (t + k) % (2 * nz), dp), device_id_type=MESH
-        )
-        return 0
-
     lax.fori_loop(1, ne, greet_expert, 0)
-    lax.fori_loop(1, 2 * nz, greet_tensor, 0)
+    for peer in (*sides, other):
+        pl.semaphore_signal(barrier, inc=1, device_id=peer, device_id_type=MESH)
     pl.semaphore_signal(barrier, inc=1, device_id=mate, device_id_type=MESH)
     local(xr_ref, xt.at[:, cols(z, 0)], loc_sem)
     for i, (src, dst) in enumerate(((wru_hbm, wru), (wrd_hbm, wrd), (wfu_hbm, wfu), (wfd_hbm, wfd))):
@@ -210,7 +213,7 @@
         return 0
 
     lax.fori_loop(0, total // chunk, real_slots, 0)
-    pl.semaphore_wait(barrier, 2 * (ne - 1) + 2 * nz)
+    pl.semaphore_wait(barrier, 2 * (ne - 1) + 4)
 
     def ring_send(ref, zz, sub, way, dist, send, recv):
         remote(
@@ -236,146 +239,233 @@
         ring_send(xt, z, 0, way, 1, xt_send, xt_recv)
     remote(xt.at[:, cols(z, 0)], xt.at[:, cols(z, 0)], xt_send, xt_yh, other)
 
-    def fake_give(i, src, dst):
-        for far, y in ((0, yh), (1, oy)):
-
-            def give(k, _, far=far, y=y):
-                to = (e + k) % ne
-                remote(
-                    src.at[block(to), :],
-                    dst.at[block(e), cols(z, 0)],
-                    fd_send.at[i, far],
-                    fd_recv.at[i, far],
-                    (to, y * nz + z, dp),
-                )
-                return 0
-
-            lax.fori_loop(1 - far, ne, give, 0)
-        local(src.at[block(e), :], dst.at[block(e), cols(z, 0)], fd_recv.at[i, 0])
-
-    fake_give(0, sx, xf)
+    def fake_give(i, src, dst, far):
+        y = oy if far else yh
+
+        def give(k, _):
+            to = (e + k) % ne
+            remote(
+                src.at[block(to), :],
+                dst.at[block(e), cols(z, 0)],
+                fd_send.at[i, far],
+                fd_recv.at[i, far],
+                (to, y * nz + z, dp),
+            )
+            return 0
+
+        lax.fori_loop(1 - far, ne, give, 0)
+        if not far:
+            local(src.at[block(e), :], dst.at[block(e), cols(z, 0)], fd_recv.at[i, 0])
+
+    fake_give(0, sx, xf, 0)
 
     def slot(zz, sub):
         sent[:, cols(zz, sub)] = jnp.dot(
             spread[...], xt[:, cols(zz, sub)], preferred_element_type=F32
         ).astype(BF)
 
-    def dispatch(zz, sub):
-        def give(k, _):
-            to = (e + k) % ne
-            remote(
-                sent.at[block(to), cols(zz, sub)],
-                rows.at[block(e), cols(zz, sub)],
-                rd_send,
-                rd_recv,
-                (to, t, dp),
+    def pair_of(dist):
+        return (near(dist),) if dist in (0, nz // 2) else (near(-dist), near(dist))
+
+    def share(expert, part):
+        if part is None:
+            return block(expert)
+        return pl.ds(pl.multiple_of(expert * cap + part * (cap // 2), cap // 2), cap // 2)
+
+    def dispatch(dist, sub, part=None):
+        for n, zz in enumerate(pair_of(dist)):
+            recv = rd_recv.at[dist, n, sub] if part is None else rh_recv.at[dist, n, part]
+
+            def give(k, _, zz=zz, recv=recv):
+                to = (e + k) % ne
+                remote(
+                    sent.at[share(to, part), cols(zz, sub)],
+                    rows.at[share(e, part), cols(zz, sub)],
+                    rd_send,
+                    recv,
+                    (to, t, dp),
+                )
+                return 0
+
+            lax.fori_loop(1, ne, give, 0)
+            local(
+                sent.at[share(e, part), cols(zz, sub)], rows.at[share(e, part), cols(zz, sub)], recv
             )
-            return 0
-
-        lax.fori_loop(1, ne, give, 0)
+
+    late = (2, 3, 4)
 
     def real_step(dist, sub):
         ring_take(xt, dist, sub, xt_send, xt_recv)
-        if dist == nz // 2:
-            slot(near(dist), sub)
-            dispatch(near(dist), sub)
-        else:
-            slot(near(-dist), sub)
-            slot(near(dist), sub)
-            dispatch(near(-dist), sub)
-            dispatch(near(dist), sub)
+        for zz in pair_of(dist):
+            slot(zz, sub)
+        dispatch(dist, sub, 0 if sub == 1 and dist in late else None)
+
+    def up_part(dist, sub):
+        where = [cols(zz, sub) for zz in pair_of(dist)]
+        for n, zz in enumerate(pair_of(dist)):
+            landed(rows.at[:, cols(zz, sub)], rd_recv.at[dist, n, sub])
+        w = jnp.concatenate([wru[c, :] for c in where], axis=0)
+
+        def part(r, _):
+            at = pl.ds(pl.multiple_of(r * chunk, chunk), chunk)
+            got = jnp.concatenate([rows[at, c] for c in where], axis=1)
+            pre = jnp.dot(got, w, preferred_element_type=F32)
+            if dist == 0 and sub == 0:
+                acc[at, :] = pre
+            else:
+                acc[at, :] += pre
+            return 0
+
+        lax.fori_loop(0, total // chunk, part, 0)
+
+    def halves(r, part):
+        return [share(r * 4 + j, part) for j in range(4)]
+
+    def up_half(part):
+        where = [cols(zz, 1) for dist in late for zz in pair_of(dist)]
+        for dist in late:
+            for n, zz in enumerate(pair_of(dist)):
+                half_bytes = rows.at[pl.ds(0, total // 2), cols(zz, 1)]
+                landed(half_bytes, rh_recv.at[dist, n, part])
+        w = jnp.concatenate([wru[c, :] for c in where], axis=0)
+
+        def some(r, _):
+            ats = halves(r, part)
+            got = jnp.concatenate(
+                [jnp.concatenate([rows[at, c] for c in where], axis=1) for at in ats], axis=0
+            )
+            pre = jnp.dot(got, w, preferred_element_type=F32)
+            for j, at in enumerate(ats):
+                own = acc[at, :] + pre[j * (cap // 2) : (j + 1) * (cap // 2), :]
+                hidden[at, :] = gelu_tanh(own).astype(BF)
+            return 0
+
+        lax.fori_loop(0, ne // 4, some, 0)
+
+    fakes = ((0, xf), (1, df))
+
+    def fake_own(i, ref, sub):
+        landed(ref.at[:, cols(z, sub)], fd_recv.at[i, sub])
+        for way in (0, 1):
+            ring_send(ref, z, sub, way, 1, f_send.at[i], f_recv.at[i])
+
+    def fake_step(i, ref, dist, sub):
+        ring_take(ref, dist, sub, f_send.at[i], f_recv.at[i])
+
+    def fake_up(r, _):
+        at = pl.ds(pl.multiple_of(r * chunk, chunk), chunk)
+        pre = jnp.dot(xf[at, :], wfu[...], preferred_element_type=F32)
+        a, s = gelu_both(pre)
+        act_t[:, at] = a.T.astype(BF)
+        slope[at, :] = s
+        return 0
+
+    theirs = pl.ds(pl.multiple_of((1 - dp) * wide, 128), wide)
 
     slot(z, 0)
+    dispatch(0, 0)
+    real_step(1, 0)
+    fake_give(0, sx, xf, 1)
+    real_step(2, 0)
+    fake_own(0, xf, 0)
+    real_step(3, 0)
     landed(xt.at[:, cols(z, 1)], xt_yh)
     for way in (0, 1):
         ring_send(xt, z, 1, way, 1, xt_send, xt_recv)
     slot(z, 1)
-    dispatch(z, 0)
-    dispatch(z, 1)
-
-    fakes = ((0, xf), (1, df))
-
-    def fake_own(i, ref, sub):
-        landed(ref.at[:, cols(z, sub)], fd_recv.at[i, sub])
-        for way in (0, 1):
-            ring_send(ref, z, sub, way, 1, f_send.at[i], f_recv.at[i])
-
-    def fake_step(i, ref, dist, sub):
-        ring_take(ref, dist, sub, f_send.at[i], f_recv.at[i])
-
-    for dist in (1, 2, 3):
-        real_step(dist, 0)
-        real_step(dist, 1)
-    fake_own(0, xf, 0)
+    dispatch(0, 1)
+    real_step(1, 1)
+    real_step(4, 0)
     fake_own(0, xf, 1)
-    real_step(4, 0)
+    real_step(2, 1)
+    fake_step(0, xf, 1, 0)
+    fake_give(1, sd, df, 0)
+    fake_give(1, sd, df, 1)
+    real_step(3, 1)
     real_step(4, 1)
-    local(sent.at[block(e), :], rows.at[block(e), :], rd_recv)
-    fake_give(1, sd, df)
+    for dist in late:
+        dispatch(dist, 1, 1)
     weights = wt[...].T
     rounded = weights.astype(BF)
     high[...] = rounded
     low[...] = (weights - rounded.astype(F32)).astype(BF)
-    fake_step(0, xf, 1, 0)
-    fake_step(0, xf, 1, 1)
-    fake_step(0, xf, 2, 0)
-    fake_step(0, xf, 2, 1)
-    fake_step(0, xf, 3, 0)
-    fake_step(0, xf, 3, 1)
-
     for i, (src, dst) in enumerate(((wru_hbm, wru), (wrd_hbm, wrd), (wfu_hbm, wfu), (wfd_hbm, wfd))):
         pltpu.make_async_copy(src, dst, w_sem.at[i]).wait()
-    landed(rows, rd_recv)
-
-    def up(r, _):
-        at = pl.ds(pl.multiple_of(r * chunk, chunk), chunk)
-        pre = jnp.dot(rows[at, :], wru[...], preferred_element_type=F32)
-        hidden[at, :] = gelu_tanh(pre).astype(BF)
-        return 0
-
-    lax.fori_loop(0, total // chunk, up, 0)
-
+    up_part(0, 0)
+    up_part(1, 0)
+    fake_step(0, xf, 1, 1)
+    up_part(2, 0)
+    fake_step(0, xf, 2, 0)
+    up_part(3, 0)
+    up_part(4, 0)
+    up_part(0, 1)
+    fake_step(0, xf, 2, 1)
+    up_part(1, 1)
+    fake_step(0, xf, 3, 0)
+    fake_own(1, df, 0)
+    fake_own(1, df, 1)
+    up_half(0)
+
+    early = (0, 1)
     turns = [nz // 2] + [way * d for d in range(nz // 2 - 1, 0, -1) for way in (-1, 1)] + [0]
 
-    def down(step):
+    def down(step, part=None):
         zz = near(turns[step])
         w = jnp.concatenate([wrd[:, cols(zz, 0)], wrd[:, cols(zz, 1)]], axis=1)
 
-        def part(r, _):
-            at = pl.ds(pl.multiple_of(r * chunk, chunk), chunk)
-            got = jnp.dot(hidden[at, :], w, preferred_element_type=F32).astype(BF)
-            po[at, cols(zz, 0)] = got[:, :128]
-            po[at, cols(zz, 1)] = got[:, 128:]
+        def some(r, _):
+            if part is None:
+                ats = [pl.ds(pl.multiple_of(r * chunk, chunk), chunk)]
+            else:
+                ats = halves(r, part)
+            got = [hidden[at, :] for at in ats]
+            got = got[0] if part is None else jnp.concatenate(got, axis=0)
+            got = jnp.dot(got, w, preferred_element_type=F32).astype(BF)
+            size = chunk // len(ats)
+            for j, at in enumerate(ats):
+                po[at, cols(zz, 0)] = got[j * size : (j + 1) * size, :128]
+                po[at, cols(zz, 1)] = got[j * size : (j + 1) * size, 128:]
             return 0
 
-        lax.fori_loop(0, total // chunk, part, 0)
-
-    def give_back(step):
+        lax.fori_loop(0, total // chunk if part is None else ne // 4, some, 0)
+
+    def give_back(step, part=None):
         zz = near(turns[step])
         for sub in (0, 1):
-
-            def give(k, _, sub=sub):
+            recv = rt_recv.at[step, sub] if part is None else rth_recv.at[step, sub, part]
+
+            def give(k, _, sub=sub, recv=recv):
                 to = (e + k) % ne
                 remote(
-                    po.at[block(to), cols(zz, sub)],
-                    ret.at[block(e), cols(zz, sub)],
+                    po.at[share(to, part), cols(zz, sub)],
+                    ret.at[share(e, part), cols(zz, sub)],
                     rt_send,
-                    rt_recv.at[step, sub],
+                    recv,
                     (to, t, dp),
                 )
                 return 0
 
             lax.fori_loop(1, ne, give, 0)
-            local(po.at[block(e), cols(zz, sub)], ret.at[block(e), cols(zz, sub)], rt_recv.at[step, sub])
-
-    down(0)
-    for step in range(1, nz):
+            local(
+                po.at[share(e, part), cols(zz, sub)], ret.at[share(e, part), cols(zz, sub)], recv
+            )
+
+    for step in early:
+        down(step, 0)
+    for step in early:
+        give_back(step, 0)
+    fake_step(0, xf, 3, 1)
+    up_half(1)
+    for step in early:
+        down(step, 1)
+    for step in early:
+        give_back(step, 1)
+    down(len(early))
+    for step in range(len(early) + 1, nz):
         down(step)
         give_back(step - 1)
-        if step == 2:
-            fake_own(1, df, 0)
-        if step == 5:
-            fake_own(1, df, 1)
+        if step == nz // 2:
+            fake_step(1, df, 1, 0)
     give_back(nz - 1)
 
     def combine(step):
@@ -383,7 +473,11 @@
         dist = abs(turn)
         zz = near(turn)
         for sub in (0, 1):
-            landed(ret.at[:, cols(zz, sub)], rt_recv.at[step, sub])
+            if step in early:
+                for part in (0, 1):
+                    landed(ret.at[pl.ds(0, total // 2), cols(zz, sub)], rth_recv.at[step, sub, part])
+            else:
+                landed(ret.at[:, cols(zz, sub)], rt_recv.at[step, sub])
         got = jnp.concatenate([ret[:, cols(zz, 0)], ret[:, cols(zz, 1)]], axis=1)
         both = jnp.dot(high[...], got, preferred_element_type=F32) + jnp.dot(
             low[...], got, preferred_element_type=F32
@@ -424,21 +518,10 @@
     def half_cols(zz, side):
         return pl.ds(pl.multiple_of(side * wide + zz * 128, 128), 128)
 
-    def fake_up(r, _):
-        at = pl.ds(pl.multiple_of(r * chunk, chunk), chunk)
-        pre = jnp.dot(xf[at, :], wfu[...], preferred_element_type=F32)
-        a, s = gelu_both(pre)
-        act_t[:, at] = a.T.astype(BF)
-        slope[at, :] = s
-        return 0
-
     def fake_mate(dist):
         for n, zz in enumerate(pair_of(dist)):
             at = pl.ds(pl.multiple_of(zz * 128, 128), 128)
             remote(df.at[:, half_cols(zz, 1 - dp)], pd.at[:, at], pd_send, pd_recv.at[dist, n], mate)
-
-    def pair_of(dist):
-        return (near(dist),) if dist in (0, nz // 2) else (near(-dist), near(dist))
 
     def back_part(dist):
         for zz in pair_of(dist):
@@ -476,57 +559,68 @@
         for n, at in enumerate(ats):
             gd_ref[:, at] = grad[:, n * 128 : (n + 1) * 128]
 
-    theirs = pl.ds(pl.multiple_of((1 - dp) * wide, 128), wide)
-
     fake_step(0, xf, 4, 0)
     fake_step(0, xf, 4, 1)
     remote(xf.at[:, theirs], px, px_send, px_recv, mate)
     lax.fori_loop(0, total // chunk, fake_up, 0)
-    fake_step(1, df, 1, 0)
-    combine(0)
+    fake_step(1, df, 1, 1)
     remote(act_t, pact_t, dp_send.at[0], dp_recv.at[0], mate)
     fake_mate(0)
-    fake_step(1, df, 1, 1)
     fake_mate(1)
-    combine(1)
+    combine(0)
     back_part(0)
     back_part(1)
-    combine(2)
+    landed(pact_t, dp_recv.at[0])
     fake_step(1, df, 2, 0)
-    landed(pact_t, dp_recv.at[0])
     grad_down_part(0)
     grad_down_part(1)
-    combine(3)
+    combine(1)
     fake_step(1, df, 2, 1)
     fake_mate(2)
-    combine(4)
+    combine(2)
     back_part(2)
+    landed(px, px_recv)
+
+    def turn_x(m, _):
+        at = pl.ds(pl.multiple_of(m * chunk, chunk), chunk)
+        own = pl.ds(pl.multiple_of(dp * wide + m * chunk, chunk), chunk)
+        xo_t[at, :] = xf[:, own].T
+        px_t[at, :] = px[:, at].T
+        return 0
+
+    lax.fori_loop(0, wide // chunk, turn_x, 0)
     fake_step(1, df, 3, 0)
-    combine(5)
     grad_down_part(2)
+    combine(3)
     fake_step(1, df, 3, 1)
     fake_mate(3)
-    combine(6)
+    combine(4)
     back_part(3)
     grad_down_part(3)
-    combine(7)
+    combine(5)
+    combine(6)
     fake_step(1, df, 4, 0)
     fake_step(1, df, 4, 1)
     fake_mate(4)
     back_part(4)
     remote(dpre, pdpre, dp_send.at[1], dp_recv.at[1], mate)
     grad_down_part(4)
-    landed(px, px_recv)
+    local(gd_ref, gd_hbm, o_sem.at[0])
     half = wide // 2
     for m in (0, 1):
-        own = pl.ds(pl.multiple_of(dp * wide + m * half, 128), half)
-        acc[m * half : (m + 1) * half, :] = over_rows(xf[:, own], dpre[...])
-    landed(last, la_recv)
-    out_ref[...] = (mine_f[...] + last[...].astype(F32)).astype(BF)
+        at = slice(m * half, (m + 1) * half)
+        acc[at, :] = jnp.dot(xo_t[at, :], dpre[...], preferred_element_type=F32)
+    combine(7)
     landed(pdpre, dp_recv.at[1])
     for m in (0, 1):
         at = slice(m * half, (m + 1) * half)
-        gu_ref[at, :] = (acc[at, :] + over_rows(px[:, at], pdpre[...])).astype(BF)
+        gu_ref[at, :] = (
+            acc[at, :] + jnp.dot(px_t[at, :], pdpre[...], preferred_element_type=F32)
+        ).astype(BF)
+        local(gu_ref.at[at, :], gu_hbm.at[at, :], o_sem.at[1 + m])
+    landed(last, la_recv)
+    out_ref[...] = (mine_f[...] + last[...].astype(F32)).astype(BF)
+    local(out_ref, out_hbm, o_sem.at[3])
 
     most = pl.ds(0, (2 * nz - 1) * 128)
     seven = pl.ds(0, (ne - 1) * cap)
@@ -544,6 +638,26 @@
     landed(pd, pd_send)
     landed(act_t, dp_send.at[0])
     landed(dpre, dp_send.at[1])
+    landed(gd_ref, o_sem.at[0])
+    for m in (0, 1):
+        at = slice(m * half, (m + 1) * half)
+        landed(gu_ref.at[at, :], o_sem.at[1 + m])
+    landed(out_ref, o_sem.at[3])
+
+
+def settle(*refs):
+    count = 3
+    given, kept, held = refs[:count], refs[count : 2 * count], refs[2 * count : 3 * count]
+    get, put = refs[3 * count :]
+    coming = [pltpu.make_async_copy(a, v, get.at[i]) for i, (a, v) in enumerate(zip(given, held))]
+    going = [pltpu.make_async_copy(v, b, put.at[i]) for i, (v, b) in enumerate(zip(held, kept))]
+    for copy in coming:
+        copy.start()
+    for first, then in zip(coming, going):
+        first.wait()
+        then.start()
+    for copy in going:
+        copy.wait()
 
 
 def solution(mesh):
@@ -572,16 +686,22 @@
         vmem = pl.BlockSpec(memory_space=pltpu.VMEM)
         hbm = pl.BlockSpec(memory_space=pl.ANY)
         dma = pltpu.SemaphoreType.DMA
-        real_out, grad_up, grad_down = pl.pallas_call(
+        shapes = (
+            jax.ShapeDtypeStruct((tokens, part), BF),
+            jax.ShapeDtypeStruct((half, ff), BF),
+            jax.ShapeDtypeStruct((ff, half), BF),
+        )
+        results = pl.pallas_call(
             functools.partial(kernel, (ne, nz, cap)),
-            out_shape=(
-                jax.ShapeDtypeStruct((tokens, part), BF),
-                jax.ShapeDtypeStruct((half, ff), BF),
-                jax.ShapeDtypeStruct((ff, half), BF),
-            ),
+            out_shape=shapes,
             in_specs=[vmem] * 7 + [hbm] * 4,
-            out_specs=(vmem, vmem, vmem),
+            out_specs=(hbm, hbm, hbm),
             scratch_shapes=[
+                pltpu.VMEM((tokens, part), BF),
+                pltpu.VMEM((half, ff), BF),
+                pltpu.VMEM((ff, half), BF),
+                pltpu.VMEM((half, total), BF),
+                pltpu.VMEM((half, total), BF),
                 pltpu.VMEM((width, ff), BF),
                 pltpu.VMEM((ff, width), BF),
                 pltpu.VMEM((width, ff), BF),
@@ -613,6 +733,7 @@
                 pltpu.VMEM((tokens, part), F32),
                 pltpu.VMEM((tokens, part), BF),
                 dma((4,)),
+                dma((4,)),
                 dma,
                 dma,
                 dma,
@@ -622,9 +743,11 @@
                 dma((2,)),
                 dma((2, 2, nz // 2, 2)),
                 dma,
-                dma,
+                dma((nz // 2 + 1, 2, 2)),
+                dma((nz // 2 + 1, 2, 2)),
                 dma,
                 dma((nz, 2)),
+                dma((2, 2, 2)),
                 dma,
                 dma((2, nz // 2)),
                 dma,
@@ -652,6 +775,13 @@
             up_fake[0],
             down_fake[0],
         )
+        real_out, grad_up, grad_down = pl.pallas_call(
+            settle,
+            out_shape=shapes,
+            in_specs=[hbm] * 3,
+            out_specs=(hbm,) * 3,
+            scratch_shapes=[pltpu.VMEM(a.shape, a.dtype) for a in shapes] + [dma((3,)), dma((3,))],
+        )(*results)
         return real_out, grad_up[None], grad_down[None]
 
     placed = (

time: 139 us -> 135 us (0.971)
  local copies, waits for them, and re-layouts: 4.8 us -> 0 us
    unnamed x5 -> x0, local copies, waits for them, and re-layouts: 4.8 us -> none
    pallas_call x1 -> x2, Pallas kernels: 133 us -> 133 us  [the longest x1 131 us: on_device(): pl.pallas_call(functools.partial(kernel, (ne, nz, cap)), out_shape=shapes...]
where the time goes in v4:
time: 135 us; the launch traced here: 134 us
  Pallas kernels  133 us (99%)
    pallas_call x1, Pallas kernels, on_device(): pl.pallas_call(functools.partial(kernel, (ne, nz, cap)), out_shape=shapes...  131 us

profile of v4, /device:TPU:6, one launch (start us, length us, event | category | flops | bytes accessed | tf_op | source)
XLA Modules:
  0.0 134.3 jit_solution(11811574923767767339)
XLA Ops:
  0.6 130.8 %shard_map.130 = (bf16[256,128]{1,0:T(8,128)(2,1)}, bf16[1024,512]{1,0:T(8,128)(2,1)}, bf16[512,1024]{1,0:T(8,128)(2,1)}) custom-call(bf16[256,128]{1,0:T(8,128)(2,1)} %xr_ref.1, bf16[256,128]{1,0:T(8,128)(2,1)} %xk_ref.1, bf16[256,128]{1,0:T(8,128)(2,1)} %ct_ref.1, s32[2,256]{1,0:T(2,128)} %bitcast.14, f32[2,256]{1,0:T(2,128)} %bitcast.15, ...), custom_call_target="tpu_custom_call" | custom-call | tf_op jit(solution)/shard_map/pallas_call | solution.py:694
  131.5 2.6 %shard_map.131 = (bf16[256,128]{1,0:T(8,128)(2,1)}, bf16[1024,512]{1,0:T(8,128)(2,1)}, bf16[512,1024]{1,0:T(8,128)(2,1)}) custom-call(bf16[256,128]{1,0:T(8,128)(2,1)} %get-tuple-element.9.refs_0_, bf16[1024,512]{1,0:T(8,128)(2,1)} %get-tuple-element.10.refs_1_, bf16[512,1024]{1,0:T(8,128)(2,1)} %get-tuple-element.11.refs_2_), custom_call_target="tpu_custom_call" | custom-call | tf_op jit(solution)/shard_map/pallas_call | solution.py:778

commit v5 on v4

--- a/solution.py
+++ b/solution.py
@@ -37,13 +37,13 @@
 
 def kernel(
     sizes,
-    xr_ref,
-    xk_ref,
-    ct_ref,
-    rr_ref,
-    gr_ref,
-    rf_ref,
-    gf_ref,
+    xr_in,
+    xk_in,
+    ct_in,
+    rr_in,
+    gr_in,
+    rf_in,
+    gf_in,
     wru_hbm,
     wrd_hbm,
     wfu_hbm,
@@ -56,6 +56,13 @@
     gd_ref,
     xo_t,
     px_t,
+    xr_ref,
+    xk_ref,
+    ct_ref,
+    rr_ref,
+    gr_ref,
+    rf_ref,
+    gf_ref,
     wru,
     wrd,
     wfu,
@@ -88,6 +95,7 @@
     last,
     w_sem,
     o_sem,
+    i_sem,
     loc_sem,
     xt_send,
     xt_yh,
@@ -148,6 +156,17 @@
     mate = (e, t, 1 - dp)
     sides = ((e, yh * nz + near(1), dp), (e, yh * nz + near(-1), dp))
 
+    inputs = (
+        (xr_in, xr_ref),
+        (xk_in, xk_ref),
+        (ct_in, ct_ref),
+        (rr_in, rr_ref),
+        (gr_in, gr_ref),
+        (rf_in, rf_ref),
+        (gf_in, gf_ref),
+    )
+    for i, (src, dst) in enumerate(inputs):
+        local(src, dst, i_sem.at[i])
     barrier = pltpu.get_barrier_semaphore()
 
     def greet_expert(k, _):
@@ -161,6 +180,8 @@
     for peer in (*sides, other):
         pl.semaphore_signal(barrier, inc=1, device_id=peer, device_id_type=MESH)
     pl.semaphore_signal(barrier, inc=1, device_id=mate, device_id_type=MESH)
+    for i, (src, dst) in enumerate(inputs):
+        pltpu.make_async_copy(src, dst, i_sem.at[i]).wait()
     local(xr_ref, xt.at[:, cols(z, 0)], loc_sem)
     for i, (src, dst) in enumerate(((wru_hbm, wru), (wrd_hbm, wrd), (wfu_hbm, wfu), (wfd_hbm, wfd))):
         local(src, dst, w_sem.at[i])
@@ -272,27 +293,38 @@
             return block(expert)
         return pl.ds(pl.multiple_of(expert * cap + part * (cap // 2), cap // 2), cap // 2)
 
+    late = (2, 3, 4)
+    flip = e + 1 - 2 * (e % 2)
+
     def dispatch(dist, sub, part=None):
+        def send(at, to, y, part, recv):
+            remote(
+                sent.at[share(to, part), at], rows.at[share(e, part), at], rd_send, recv, (to, y * nz + z, dp)
+            )
+
         for n, zz in enumerate(pair_of(dist)):
+            at = cols(zz, sub)
             recv = rd_recv.at[dist, n, sub] if part is None else rh_recv.at[dist, n, part]
 
-            def give(k, _, zz=zz, recv=recv):
-                to = (e + k) % ne
-                remote(
-                    sent.at[share(to, part), cols(zz, sub)],
-                    rows.at[share(e, part), cols(zz, sub)],
-                    rd_send,
-                    recv,
-                    (to, t, dp),
-                )
+            def along(k, _, at=at, recv=recv):
+                send(at, (e + 2 * k) % ne, yh, part, recv)
                 return 0
 
-            lax.fori_loop(1, ne, give, 0)
-            local(
-                sent.at[share(e, part), cols(zz, sub)], rows.at[share(e, part), cols(zz, sub)], recv
-            )
-
-    late = (2, 3, 4)
+            lax.fori_loop(1, ne // 2, along, 0)
+            local(sent.at[share(e, part), at], rows.at[share(e, part), at], recv)
+            if sub == 0:
+
+                def across(k, _, at=at, recv=recv, n=n):
+                    to = (flip + 2 * k) % ne
+                    send(at, to, yh, None, recv)
+                    if dist in late:
+                        for half in (0, 1):
+                            send(at, to, oy, half, rh_recv.at[dist, n, half])
+                    else:
+                        send(at, to, oy, None, rd_recv.at[dist, n, 1])
+                    return 0
+
+                lax.fori_loop(0, ne // 2, across, 0)
 
     def real_step(dist, sub):
         ring_take(xt, dist, sub, xt_send, xt_recv)
@@ -432,22 +464,35 @@
     def give_back(step, part=None):
         zz = near(turns[step])
         for sub in (0, 1):
-            recv = rt_recv.at[step, sub] if part is None else rth_recv.at[step, sub, part]
-
-            def give(k, _, sub=sub, recv=recv):
-                to = (e + k) % ne
+
+            def recv(sub):
+                return rt_recv.at[step, sub] if part is None else rth_recv.at[step, sub, part]
+
+            def send(to, y, sub, into):
                 remote(
                     po.at[share(to, part), cols(zz, sub)],
                     ret.at[share(e, part), cols(zz, sub)],
                     rt_send,
-                    recv,
-                    (to, t, dp),
+                    recv(into),
+                    (to, y * nz + z, dp),
                 )
+
+            def along(k, _, sub=sub):
+                send((e + 2 * k) % ne, yh, sub, sub)
                 return 0
 
-            lax.fori_loop(1, ne, give, 0)
+            def across(k, _, sub=sub):
+                to = (flip + 2 * k) % ne
+                if step % 2 == 0:
+                    send(to, yh, sub, sub)
+                else:
+                    send(to, oy, sub, 1 - sub)
+                return 0
+
+            lax.fori_loop(1, ne // 2, along, 0)
+            lax.fori_loop(0, ne // 2, across, 0)
             local(
-                po.at[share(e, part), cols(zz, sub)], ret.at[share(e, part), cols(zz, sub)], recv
+                po.at[share(e, part), cols(zz, sub)], ret.at[share(e, part), cols(zz, sub)], recv(sub)
             )
 
     for step in early:
@@ -464,8 +509,6 @@
     for step in range(len(early) + 1, nz):
         down(step)
         give_back(step - 1)
-        if step == nz // 2:
-            fake_step(1, df, 1, 0)
     give_back(nz - 1)
 
     def combine(step):
@@ -559,6 +602,7 @@
         for n, at in enumerate(ats):
             gd_ref[:, at] = grad[:, n * 128 : (n + 1) * 128]
 
+    fake_step(1, df, 1, 0)
     fake_step(0, xf, 4, 0)
     fake_step(0, xf, 4, 1)
     remote(xf.at[:, theirs], px, px_send, px_recv, mate)
@@ -592,25 +636,25 @@
     fake_step(1, df, 3, 0)
     grad_down_part(2)
     combine(3)
+    combine(4)
     fake_step(1, df, 3, 1)
     fake_mate(3)
-    combine(4)
     back_part(3)
+    combine(5)
     grad_down_part(3)
-    combine(5)
     combine(6)
     fake_step(1, df, 4, 0)
     fake_step(1, df, 4, 1)
     fake_mate(4)
     back_part(4)
     remote(dpre, pdpre, dp_send.at[1], dp_recv.at[1], mate)
+    combine(7)
     grad_down_part(4)
     local(gd_ref, gd_hbm, o_sem.at[0])
     half = wide // 2
     for m in (0, 1):
         at = slice(m * half, (m + 1) * half)
         acc[at, :] = jnp.dot(xo_t[at, :], dpre[...], preferred_element_type=F32)
-    combine(7)
     landed(pdpre, dp_recv.at[1])
     for m in (0, 1):
         at = slice(m * half, (m + 1) * half)
@@ -683,7 +727,6 @@
         width = up_real.shape[1]
         ff = up_real.shape[2]
         half = width // 2
-        vmem = pl.BlockSpec(memory_space=pltpu.VMEM)
         hbm = pl.BlockSpec(memory_space=pl.ANY)
         dma = pltpu.SemaphoreType.DMA
         shapes = (
@@ -694,7 +737,7 @@
         results = pl.pallas_call(
             functools.partial(kernel, (ne, nz, cap)),
             out_shape=shapes,
-            in_specs=[vmem] * 7 + [hbm] * 4,
+            in_specs=[hbm] * 11,
             out_specs=(hbm, hbm, hbm),
             scratch_shapes=[
                 pltpu.VMEM((tokens, part), BF),
@@ -702,6 +745,13 @@
                 pltpu.VMEM((ff, half), BF),
                 pltpu.VMEM((half, total), BF),
                 pltpu.VMEM((half, total), BF),
+                pltpu.VMEM((tokens, part), BF),
+                pltpu.VMEM((tokens, part), BF),
+                pltpu.VMEM((tokens, part), BF),
+                pltpu.VMEM((2, tokens), jnp.int32),
+                pltpu.VMEM((2, tokens), F32),
+                pltpu.VMEM((2, tokens), jnp.int32),
+                pltpu.VMEM((2, tokens), F32),
                 pltpu.VMEM((width, ff), BF),
                 pltpu.VMEM((ff, width), BF),
                 pltpu.VMEM((width, ff), BF),
@@ -734,6 +784,7 @@
                 pltpu.VMEM((tokens, part), BF),
                 dma((4,)),
                 dma((4,)),
+                dma((7,)),
                 dma,
                 dma,
                 dma,

time: 135 us -> 133 us (0.985); the launches traced: 134 us -> 131 us
  Pallas kernels: 133 us -> 130 us
    pallas_call x1, Pallas kernels: 131 us -> 127 us  [on_device(): pl.pallas_call(functools.partial(kernel, (ne, nz, cap)), out_shape=shapes...]
where the time goes in v5:
time: 133 us; the launch traced here: 131 us
  Pallas kernels  130 us (98%)
    pallas_call x1, Pallas kernels, on_device(): pl.pallas_call(functools.partial(kernel, (ne, nz, cap)), out_shape=shapes...  127 us

profile of v5, /device:TPU:6, one launch (start us, length us, event | category | flops | bytes accessed | tf_op | source)
XLA Modules:
  0.0 130.7 jit_solution(13121827025547225256)
XLA Ops:
  0.6 127.3 %shard_map.130 = (bf16[256,128]{1,0:T(8,128)(2,1)}, bf16[1024,512]{1,0:T(8,128)(2,1)}, bf16[512,1024]{1,0:T(8,128)(2,1)}) custom-call(bf16[256,128]{1,0:T(8,128)(2,1)} %xr_in.1, bf16[256,128]{1,0:T(8,128)(2,1)} %xk_in.1, bf16[256,128]{1,0:T(8,128)(2,1)} %ct_in.1, s32[2,256]{1,0:T(2,128)} %bitcast.14, f32[2,256]{1,0:T(2,128)} %bitcast.15, s32[2,256]{1,0:T(2,128)} %bitcast.16, ...), custom_call_target="tpu_custom_call" | custom-call | tf_op jit(solution)/shard_map/pallas_call | solution.py:737
  127.9 2.6 %shard_map.131 = (bf16[256,128]{1,0:T(8,128)(2,1)}, bf16[1024,512]{1,0:T(8,128)(2,1)}, bf16[512,1024]{1,0:T(8,128)(2,1)}) custom-call(bf16[256,128]{1,0:T(8,128)(2,1)} %get-tuple-element.9.refs_0_, bf16[1024,512]{1,0:T(8,128)(2,1)} %get-tuple-element.10.refs_1_, bf16[512,1024]{1,0:T(8,128)(2,1)} %get-tuple-element.11.refs_2_), custom_call_target="tpu_custom_call" | custom-call | tf_op jit(solution)/shard_map/pallas_call | solution.py:829
